TPU v7x, 512 devices: a 8x2x16 block of a 8x8x16 slice. The times are simulated.
512 devices in a mesh: group: 2 (over y), plane: 16 (over z), planey: 8 (over x), ens: 2 (over core).
Axes of the slice: x: 8, y: 2, z: 16, core: 2. Of those that a mesh axis runs over, the one named last changes fastest.
The devices are a block of a 8x8x16 slice.
Arguments:
- u_prior: float32 [8, 2, 10, 256, 1024], P(('group', 'ens'), None, None, 'plane', 'planey'), parts along dimension 0, may hold values from -6 to 6
- friction_rows: int32 [8], P(('group', 'ens')), parts along dimension 0, may hold values from 0 to 15
- friction_table: float32 [32, 256, 1024], P('group', 'plane', 'planey'), parts along dimension 0, may hold values from 0.3 to 3
- bed_fixed: int32 [256, 1024], P('plane', 'planey'), may hold values from -536870912 to 536870911
- ice_mask: int32 [256, 1024], P('plane', 'planey'), may hold values 0 or 1
Outputs:
- mean_velocity: float32 [4, 10, 256, 1024], P('group', None, 'plane', 'planey'), parts along dimension 0
There are 2 independent parts, one for each index of `group`. A program takes and returns all parts, laid end to end along the dimension named above; an argument that names none is the same for every part. Nothing has to cross between parts.
Inputs may be any that keep to these rules, and one draw needn't show every extreme that they name: `friction_rows`: each sample names one row of the friction table.
All inputs are finite; a program needn't handle non-finite values. No bound on the sum of `ice_mask` on one device may be relied on, other than what follows from the above.
Results may differ from a plain program's by a relative error of at most 0.0003.
Values sent between devices are 32-bit elements; how exact they have to be, the bound alone decides.
A program may use at most 64 MiB of HBM per device.

v0:
```python
import jax
import jax.numpy as jnp
from jax import lax
from jax.sharding import PartitionSpec as P

bed_unit = 2.0 ** (-29)
factor_u = (2.0, 1.0, 0.5)
factor_v = (2.0, 0.5, 1.0)


def extended_2(cells, sides, width):
    for axis, dim in sides:
        count = lax.axis_size(axis)
        ends = count - 1
        head = lax.slice_in_dim(cells, 0, width, axis=dim)
        tail = lax.slice_in_dim(cells, cells.shape[dim] - width, cells.shape[dim], axis=dim)
        cells = jnp.concatenate(
            [
                lax.ppermute(tail, axis, [(i, (i + 1) % count) for i in range(ends)]),
                cells,
                lax.ppermute(head, axis, [((i + 1) % count, i) for i in range(ends)]),
            ],
            axis=dim,
        )
    return cells


def one_axis_at_a_time(value, axes):
    for axis in axes:
        value = lax.psum(value, axis)
    return value


def total_of_pieces(value, axis):
    blocks = lax.all_gather(value, axis)
    return blocks.sum(axis=0)


def coefficient(offset):
    nonzero = len([entry for entry in offset if entry != 0])
    weight_u = 0.25 ** (nonzero - 1)
    weight_v = weight_u
    for dimension in range(3):
        if offset[dimension] != 0:
            weight_u = weight_u * factor_u[dimension]
            weight_v = weight_v * factor_v[dimension]
    return jnp.array([weight_u, weight_v], jnp.float32).reshape(2, 1, 1, 1)


def neighbour_sum(padded):
    layers = padded.shape[-3] - 2
    span_x = padded.shape[-2] - 2
    span_y = padded.shape[-1] - 2
    summed = None
    for step_z in (-1, 0, 1):
        for step_x in (-1, 0, 1):
            for step_y in (-1, 0, 1):
                if step_z == 0 and step_x == 0 and (step_y == 0):
                    continue
                window = padded[
                    ...,
                    1 + step_z : 1 + step_z + layers,
                    1 + step_x : 1 + step_x + span_x,
                    1 + step_y : 1 + step_y + span_y,
                ]
                addend = coefficient((step_z, step_x, step_y)) * window
                summed = addend if summed is None else summed + addend
    return summed


def strain_roots(extended):
    padded = jnp.pad(extended, [(0, 0)] * (extended.ndim - 3) + [(1, 1), (0, 0), (0, 0)])
    along_x = (padded[..., 1:-1, 2:, 1:-1] - padded[..., 1:-1, :-2, 1:-1]) * 0.5
    along_y = (padded[..., 1:-1, 1:-1, 2:] - padded[..., 1:-1, 1:-1, :-2]) * 0.5
    along_z = (padded[..., 2:, 1:-1, 1:-1] - padded[..., :-2, 1:-1, 1:-1]) * 0.5
    stretch_x = along_x[..., 0, :, :, :]
    stretch_y = along_y[..., 1, :, :, :]
    shear_one = along_y[..., 0, :, :, :]
    shear_two = along_x[..., 1, :, :, :]
    vertical_u = along_z[..., 0, :, :, :]
    vertical_v = along_z[..., 1, :, :, :]
    shear = shear_one + shear_two
    strain = (
        stretch_x * stretch_x
        + stretch_y * stretch_y
        + stretch_x * stretch_y
        + 0.25 * shear * shear
        + 0.25 * (vertical_u * vertical_u + vertical_v * vertical_v)
    )
    return jnp.power(strain + 0.1, -1.0 / 6.0)[..., None, :, :, :]


def pad_layers(field):
    return jnp.pad(field, ((0, 0), (0, 0), (1, 1), (0, 0), (0, 0)))


def inner(left, right):
    return jnp.sum(left * right, axis=(1, 2, 3, 4))


def spread(values):
    return values.reshape(-1, 1, 1, 1, 1)


def trimmed(field, margin):
    return field[..., margin:-margin, margin:-margin]


def apply_local(roots_wide, across_part, diag_part, field_wide):
    product = roots_wide * field_wide
    nearby = neighbour_sum(pad_layers(product))
    centre = trimmed(field_wide, 1)
    return trimmed(roots_wide, 1) * (across_part * centre - nearby) + diag_part * centre


def body(u_prior, friction_rows, friction_table, bed_fixed, ice_mask):
    members = u_prior.shape[0]
    layers = u_prior.shape[2]
    rows_x = u_prior.shape[3]
    rows_y = u_prior.shape[4]
    total_x = rows_x * lax.axis_size("plane")
    cover = ice_mask.astype(jnp.float32)
    bed_block = (bed_fixed.astype(jnp.float32) * bed_unit).reshape(1, 1, 1, rows_x, rows_y)
    levels = jnp.arange(friction_table.shape[0], dtype=jnp.int32)
    chosen = (friction_rows[:, None] == levels[None, :]).astype(jnp.float32)
    friction = jnp.sum(chosen[:, :, None, None] * friction_table[None], axis=1)
    bottom = (
        (jnp.arange(layers, dtype=jnp.int32) == 0).astype(jnp.float32).reshape(1, 1, layers, 1, 1)
    )
    mask_block = cover.reshape(1, 1, 1, rows_x, rows_y)
    friction_block = friction.reshape(members, 1, 1, rows_x, rows_y)
    prior_wide, bed_wide, mask_wide, friction_wide = (
        extended_2(u_prior, (("plane", 3), ("planey", 4)), 4),
        extended_2(bed_block, (("plane", 3), ("planey", 4)), 4),
        extended_2(mask_block, (("plane", 3), ("planey", 4)), 4),
        extended_2(friction_block, (("plane", 3), ("planey", 4)), 4),
    )
    roots_three = trimmed(mask_wide, 1) * strain_roots(prior_wide)
    across_two = neighbour_sum(pad_layers(roots_three))
    bed_three = trimmed(bed_wide, 1)
    slope_x = (bed_three[..., 2:, 1:-1] - bed_three[..., :-2, 1:-1]) * 0.5
    slope_y = (bed_three[..., 1:-1, 2:] - bed_three[..., 1:-1, :-2]) * 0.5
    mask_two = trimmed(mask_wide, 2)
    position = (
        lax.axis_index("plane") * rows_x - 2 + jnp.arange(rows_x + 4, dtype=jnp.int32)
    ).astype(jnp.float32)
    thickness = 1.0 + 2.0 * position[:, None] / (total_x - 1)
    force_two = jnp.concatenate(
        [-(mask_two * thickness * slope_x), -(mask_two * thickness * slope_y)], axis=1
    )
    diag_two = mask_two * trimmed(friction_wide, 2) * bottom + (1.0 - mask_two)
    start_three = trimmed(prior_wide, 1) * trimmed(mask_wide, 1)
    residual_two = force_two - apply_local(roots_three, across_two, diag_two, start_three)
    image_one = apply_local(
        trimmed(roots_three, 1), trimmed(across_two, 1), trimmed(diag_two, 1), residual_two
    )
    second_image = apply_local(
        trimmed(roots_three, 2), trimmed(across_two, 2), trimmed(diag_two, 2), image_one
    )
    residual = trimmed(residual_two, 2)
    image = trimmed(image_one, 1)
    gram_rr, gram_ra, gram_aa, gram_ab = (
        one_axis_at_a_time(inner(residual, residual), ("plane", "planey")),
        one_axis_at_a_time(inner(residual, image), ("plane", "planey")),
        one_axis_at_a_time(inner(image, image), ("plane", "planey")),
        one_axis_at_a_time(inner(image, second_image), ("plane", "planey")),
    )
    first_step = gram_rr / gram_ra
    norm_next = gram_rr - 2.0 * first_step * gram_ra + first_step * first_step * gram_aa
    growth = 1.0 + norm_next / gram_rr
    curve = (
        growth * growth * gram_ra
        - 2.0 * growth * first_step * gram_aa
        + first_step * first_step * gram_ab
    )
    second_step = norm_next / curve
    solution = trimmed(start_three, 3)
    solution = (
        solution
        + spread(first_step + second_step * growth) * residual
        - spread(second_step * first_step) * image
    )
    local_sum = jnp.sum(solution, axis=0)
    summed = total_of_pieces(local_sum, "ens")
    return summed / (members * lax.axis_size("ens"))


def solution(mesh):
    in_specs = (
        P(("group", "ens"), None, None, "plane", "planey"),
        P(("group", "ens")),
        P("group", "plane", "planey"),
        P("plane", "planey"),
        P("plane", "planey"),
    )
    out_specs = P("group", None, "plane", "planey")
    return jax.shard_map(body, mesh=mesh, in_specs=in_specs, out_specs=out_specs, check_vma=False)
```

profile of v0, /device:TPU:80, one launch (start us, length us, event | category | flops | bytes accessed | tf_op | source)
XLA Modules:
  0.0 187.1 jit_solution(14085209569929018749)
XLA Ops:
  0.7 6.0 %collective-permute-start.4 = (f32[1,1,1,4,128]{4,3,2,1,0:T(4,128)S(1)}, f32[1,1,1,4,128]{4,3,2,1,0:T(4,128)S(1)}, u32[]{:S(2)}, u32[]{:S(2)}) collective-permute-start(f32[1,1,1,4,128]{4,3,2,1,0:T(4,128)S(1)} %get-tuple-element.76), channel_id=1, source_target_pairs={{0,16},{16,32},{32,48},{48,64},{64,80},{80,96},{96,112},{112,128},... | collective-permute-start | bytes 6152 | tf_op jit(solution)/shard_map/ppermute | solution.py:19
  6.7 1.3 collective-permute-start.5
  8.8 6.7 %collective-permute-start.8 = (f32[1,1,1,4,128]{4,3,2,1,0:T(4,128)S(1)}, f32[1,1,1,4,128]{4,3,2,1,0:T(4,128)S(1)}, u32[]{:S(2)}, u32[]{:S(2)}) collective-permute-start(f32[1,1,1,4,128]{4,3,2,1,0:T(4,128)S(1)} %get-tuple-element.74), channel_id=1, source_target_pairs={{0,16},{16,32},{32,48},{48,64},{64,80},{80,96},{96,112},{112,128},... | collective-permute-start | bytes 6152 | tf_op jit(solution)/shard_map/ppermute | solution.py:19
  15.4 1.3 collective-permute-start.9
  18.5 6.7 %collective-permute-start.12 = (f32[2,1,1,4,128]{4,3,0,2,1:T(4,128)S(1)}, f32[2,1,1,4,128]{4,3,0,2,1:T(4,128)S(1)}, u32[]{:S(2)}, u32[]{:S(2)}) collective-permute-start(f32[2,1,1,4,128]{4,3,0,2,1:T(4,128)S(1)} %get-tuple-element.68), channel_id=1, source_target_pairs={{0,16},{16,32},{32,48},{48,64},{64,80},{80,96},{96,112},{112,128},... | collective-permute-start | bytes 12296 | tf_op jit(solution)/shard_map/ppermute | solution.py:19
  27.6 7.9 %collective-permute-start = (f32[2,2,10,4,128]{4,3,2,1,0:T(4,128)S(1)}, f32[2,2,10,4,128]{4,3,2,1,0:T(4,128)S(1)}, u32[]{:S(2)}, u32[]{:S(2)}) collective-permute-start(f32[2,2,10,4,128]{4,3,2,1,0:T(4,128)S(1)} %get-tuple-element.60), channel_id=1, source_target_pairs={{0,16},{16,32},{32,48},{48,64},{64,80},{80,96},{96,112},{112,128},... | collective-permute-start | bytes 245768 | tf_op jit(solution)/shard_map/ppermute | solution.py:19
  35.6 3.6 %collective-permute-start.6 = (f32[1,1,1,24,4]{4,3,2,1,0:T(8,128)S(1)}, f32[1,1,1,24,4]{4,3,2,1,0:T(8,128)S(1)}, u32[]{:S(2)}, u32[]{:S(2)}) collective-permute-start(f32[1,1,1,24,4]{4,3,2,1,0:T(8,128)S(1)} %get-tuple-element.72), channel_id=1, source_target_pairs={{0,2},{2,4},{4,6},{6,8},{8,10},{10,12},{12,14},{1,3},{3,5},{5,7},{... | collective-permute-start | bytes 1160 | tf_op jit(solution)/shard_map/ppermute | solution.py:19
  40.5 4.6 %collective-permute-start.10 = (f32[1,1,1,24,4]{4,3,2,1,0:T(8,128)S(1)}, f32[1,1,1,24,4]{4,3,2,1,0:T(8,128)S(1)}, u32[]{:S(2)}, u32[]{:S(2)}) collective-permute-start(f32[1,1,1,24,4]{4,3,2,1,0:T(8,128)S(1)} %get-tuple-element.70), channel_id=1, source_target_pairs={{0,2},{2,4},{4,6},{6,8},{8,10},{10,12},{12,14},{1,3},{3,5},{5,7},{... | collective-permute-start | bytes 1160 | tf_op jit(solution)/shard_map/ppermute | solution.py:19
  47.9 2.9 %collective-permute-done.11 = f32[1,1,1,24,4]{4,3,2,1,0:T(8,128)S(1)} collective-permute-done((f32[1,1,1,24,4]{4,3,2,1,0:T(8,128)S(1)}, f32[1,1,1,24,4]{4,3,2,1,0:T(8,128)S(1)}, u32[]{:S(2)}, u32[]{:S(2)}) %collective-permute-start.11) | collective-permute-done | bytes 416 | tf_op jit(solution)/shard_map/ppermute | solution.py:21
  51.1 4.0 %collective-permute-start.14 = (f32[2,1,1,24,4]{4,3,0,2,1:T(8,128)S(1)}, f32[2,1,1,24,4]{4,3,0,2,1:T(8,128)S(1)}, u32[]{:S(2)}, u32[]{:S(2)}) collective-permute-start(f32[2,1,1,24,4]{4,3,0,2,1:T(8,128)S(1)} %get-tuple-element.66), channel_id=1, source_target_pairs={{0,2},{2,4},{4,6},{6,8},{8,10},{10,12},{12,14},{1,3},{3,5},{5,7},{... | collective-permute-start | bytes 2312 | tf_op jit(solution)/shard_map/ppermute | solution.py:19
  56.6 5.5 %collective-permute-done.15 = f32[2,1,1,24,4]{4,3,0,2,1:T(8,128)S(1)} collective-permute-done((f32[2,1,1,24,4]{4,3,0,2,1:T(8,128)S(1)}, f32[2,1,1,24,4]{4,3,0,2,1:T(8,128)S(1)}, u32[]{:S(2)}, u32[]{:S(2)}) %collective-permute-start.15) | collective-permute-done | bytes 800 | tf_op jit(solution)/shard_map/ppermute | solution.py:21
  63.5 5.2 %collective-permute-start.2 = (f32[2,2,10,24,4]{4,3,2,1,0:T(8,128)S(1)}, f32[2,2,10,24,4]{4,3,2,1,0:T(8,128)S(1)}, u32[]{:S(2)}, u32[]{:S(2)}) collective-permute-start(f32[2,2,10,24,4]{4,3,2,1,0:T(8,128)S(1)} %get-tuple-element.58), channel_id=1, source_target_pairs={{0,2},{2,4},{4,6},{6,8},{8,10},{10,12},{12,14},{1,3},{3,5},{5,7},{... | collective-permute-start | bytes 46088 | tf_op jit(solution)/shard_map/ppermute | solution.py:19
  68.7 1.5 collective-permute-start.3
  70.3 4.7 %collective-permute-done.2 = f32[2,2,10,24,4]{4,3,2,1,0:T(8,128)S(1)} collective-permute-done((f32[2,2,10,24,4]{4,3,2,1,0:T(8,128)S(1)}, f32[2,2,10,24,4]{4,3,2,1,0:T(8,128)S(1)}, u32[]{:S(2)}, u32[]{:S(2)}) %collective-permute-start.2) | collective-permute-done | bytes 15392 | tf_op jit(solution)/shard_map/ppermute | solution.py:19
  75.0 4.5 %collective-permute-done.3 = f32[2,2,10,24,4]{4,3,2,1,0:T(8,128)S(1)} collective-permute-done((f32[2,2,10,24,4]{4,3,2,1,0:T(8,128)S(1)}, f32[2,2,10,24,4]{4,3,2,1,0:T(8,128)S(1)}, u32[]{:S(2)}, u32[]{:S(2)}) %collective-permute-start.3) | collective-permute-done | bytes 15392 | tf_op jit(solution)/shard_map/ppermute | solution.py:21
  80.0 1.3 fusion.95
  81.9 5.0 %fusion.103 = (f32[2,10,20,132]{3,2,1,0:T(8,128)S(1)}, f32[2,10,20,132]{3,2,1,0:T(8,128)}, f32[2,10,20,132]{3,2,1,0:T(8,128)}, f32[2,10,20,132]{3,2,1,0:T(8,128)...) fusion(f32[2,1,10,22,134]{4,3,2,1,0:T(8,128)S(1)} %fusion.101), kind=kLoop, calls=%fused_computation.200 | loop fusion | flops 580800 | bytes 4995840 | tf_op jit(solution)/shard_map/mul | solution.py:66
  86.9 2.6 %fusion.133 = (f32[2,10,20,132]{3,2,1,0:T(8,128)}, f32[2,10,20,132]{3,2,1,0:T(8,128)}, f32[2,10,20,132]{3,2,1,0:T(8,128)}, f32[2,10,20,132]{3,2,1,0:T(8,128)}, f...) fusion(f32[2,1,10,22,134]{4,3,2,1,0:T(8,128)S(1)} %fusion.101), kind=kLoop, calls=%fused_computation.240 | loop fusion | flops 158400 | bytes 3379200 | tf_op jit(solution)/shard_map/mul | solution.py:66
  92.0 8.9 %broadcast_multiply_fusion.2 = (f32[2,2,10,20,132]{4,3,2,1,0:T(8,128)S(1)}, f32[2,2,10,20,132]{4,3,2,1,0:T(8,128)S(1)}, f32[2,2,10,20,132]{4,3,2,1,0:T(8,128)S(1)}) fusion(f32[2,10,20,132]{3,2,1,0:T(8,128)} %get-tuple-element.57, f32[2,10,20,132]{3,2,1,0:T(8,128)S(1)} %multiply_add_fusion.1, f32[2,2,10,22,134]{4,3,2,1,0:T(8,128)S(1)} %get-tuple-element.25, ...), kind=kLoop, calls=%fused_computation.252 | loop fusion | flops 10032000 | bytes 17623040 | tf_op jit(solution)/shard_map/mul | solution.py:110
  100.9 5.9 %broadcast_multiply_fusion = (f32[2,2,10,18,130]{4,3,2,1,0:T(8,128)S(1)}, f32[2,2,10,18,130]{4,3,2,1,0:T(8,128)S(1)}) fusion(f32[2,10,18,130]{3,2,1,0:T(8,128)} %slice_bitcast_fusion.1, f32[2,10,18,130]{3,2,1,0:T(8,128)S(1)} %slice_bitcast_fusion, f32[2,2,10,20,132]{4,3,2,1,0:T(8,128)S(1)} %get-tuple-element.22, f32[2]{0:T(128)S(1)} %copy-done.5, ...), kind=kLoop, calls=%fused_computation.249 | loop fusion | flops 5335200 | bytes 12243008 | tf_op jit(solution)/shard_map/mul | solution.py:110
  106.8 1.8 multiply_reduce_fusion.1
  108.6 58.0 %all-reduce.5 = (f32[2]{0:T(128)S(1)}, f32[2]{0:T(128)S(1)}, f32[2]{0:T(128)S(1)}, f32[2]{0:T(128)S(1)}) all-reduce(f32[2]{0:T(128)S(1)} %get-tuple-element.27, f32[2]{0:T(128)S(1)} %get-tuple-element.6, f32[2]{0:T(128)S(1)} %get-tuple-element.7, ...), channel_id=1, replica_groups=mesh['group'=2,'plane'=16,'planey'=8,'ens'=2] {'plane'}, use_global_device_ids=true, to_apply=%region_11.12 | all-reduce | flops 8 | bytes 64 | tf_op jit(solution)/shard_map/psum | solution.py:30
  166.5 17.4 %all-reduce.6 = (f32[2]{0:T(128)S(1)}, f32[2]{0:T(128)S(1)}, f32[2]{0:T(128)S(1)}, f32[2]{0:T(128)S(1)}) all-reduce(f32[2]{0:T(128)S(1)} %get-tuple-element.8, f32[2]{0:T(128)S(1)} %get-tuple-element.9, f32[2]{0:T(128)S(1)} %get-tuple-element.10, ...), channel_id=1, replica_groups=mesh['group'=2,'plane'=16,'planey'=8,'ens'=2] {'planey'}, use_global_device_ids=true, to_apply=%region_12.13 | all-reduce | flops 8 | bytes 64 | tf_op jit(solution)/shard_map/psum | solution.py:30
  184.3 2.1 %all-gather = f32[4,10,16,128]{3,2,1,0:T(8,128)S(1)} all-gather(f32[2,10,16,128]{3,2,1,0:T(8,128)S(1)} %fusion.184), channel_id=2, replica_groups=mesh['group'=2,'plane'=16,'planey'=8,'ens'=2] {'ens'}, dimensions={0}, use_global_device_ids=true | all-gather | bytes 491520 | tf_op jit(solution)/shard_map/all_gather | solution.py:35
  (68 shorter events, 17.6 us)
Async XLA Ops:
  0.7 25.5 %collective-permute-start.4 = (f32[1,1,1,4,128]{4,3,2,1,0:T(4,128)S(1)}, f32[1,1,1,4,128]{4,3,2,1,0:T(4,128)S(1)}, u32[]{:S(2)}, u32[]{:S(2)}) collective-permute-start(f32[1,1,1,4,128]{4,3,2,1,0:T(4,128)S(1)} %get-tuple-element.76), channel_id=1, source_target_pairs={{0,16},{16,32},{32,48},{48,64},{64,80},{80,96},{96,112},{112,128},... | collective-permute-start | bytes 6152 | tf_op jit(solution)/shard_map/ppermute | solution.py:19
  6.7 20.8 %collective-permute-start.5 = (f32[1,1,1,4,128]{4,3,2,1,0:T(4,128)S(1)}, f32[1,1,1,4,128]{4,3,2,1,0:T(4,128)S(1)}, u32[]{:S(2)}, u32[]{:S(2)}) collective-permute-start(f32[1,1,1,4,128]{4,3,2,1,0:T(4,128)S(1)} %get-tuple-element.77), channel_id=1, source_target_pairs={{16,0},{32,16},{48,32},{64,48},{80,64},{96,80},{112,96},{128,112},... | collective-permute-start | bytes 6152 | tf_op jit(solution)/shard_map/ppermute | solution.py:21
  8.8 26.8 %collective-permute-start.8 = (f32[1,1,1,4,128]{4,3,2,1,0:T(4,128)S(1)}, f32[1,1,1,4,128]{4,3,2,1,0:T(4,128)S(1)}, u32[]{:S(2)}, u32[]{:S(2)}) collective-permute-start(f32[1,1,1,4,128]{4,3,2,1,0:T(4,128)S(1)} %get-tuple-element.74), channel_id=1, source_target_pairs={{0,16},{16,32},{32,48},{48,64},{64,80},{80,96},{96,112},{112,128},... | collective-permute-start | bytes 6152 | tf_op jit(solution)/shard_map/ppermute | solution.py:19
  15.4 23.7 %collective-permute-start.9 = (f32[1,1,1,4,128]{4,3,2,1,0:T(4,128)S(1)}, f32[1,1,1,4,128]{4,3,2,1,0:T(4,128)S(1)}, u32[]{:S(2)}, u32[]{:S(2)}) collective-permute-start(f32[1,1,1,4,128]{4,3,2,1,0:T(4,128)S(1)} %get-tuple-element.75), channel_id=1, source_target_pairs={{16,0},{32,16},{48,32},{64,48},{80,64},{96,80},{112,96},{128,112},... | collective-permute-start | bytes 6152 | tf_op jit(solution)/shard_map/ppermute | solution.py:21
  18.5 32.6 %collective-permute-start.12 = (f32[2,1,1,4,128]{4,3,0,2,1:T(4,128)S(1)}, f32[2,1,1,4,128]{4,3,0,2,1:T(4,128)S(1)}, u32[]{:S(2)}, u32[]{:S(2)}) collective-permute-start(f32[2,1,1,4,128]{4,3,0,2,1:T(4,128)S(1)} %get-tuple-element.68), channel_id=1, source_target_pairs={{0,16},{16,32},{32,48},{48,64},{64,80},{80,96},{96,112},{112,128},... | collective-permute-start | bytes 12296 | tf_op jit(solution)/shard_map/ppermute | solution.py:19
  26.2 24.8 %collective-permute-start.13 = (f32[2,1,1,4,128]{4,3,0,2,1:T(4,128)S(1)}, f32[2,1,1,4,128]{4,3,0,2,1:T(4,128)S(1)}, u32[]{:S(2)}, u32[]{:S(2)}) collective-permute-start(f32[2,1,1,4,128]{4,3,0,2,1:T(4,128)S(1)} %get-tuple-element.69), channel_id=1, source_target_pairs={{16,0},{32,16},{48,32},{64,48},{80,64},{96,80},{112,96},{128,112},... | collective-permute-start | bytes 12296 | tf_op jit(solution)/shard_map/ppermute | solution.py:21
  27.6 35.1 %collective-permute-start = (f32[2,2,10,4,128]{4,3,2,1,0:T(4,128)S(1)}, f32[2,2,10,4,128]{4,3,2,1,0:T(4,128)S(1)}, u32[]{:S(2)}, u32[]{:S(2)}) collective-permute-start(f32[2,2,10,4,128]{4,3,2,1,0:T(4,128)S(1)} %get-tuple-element.60), channel_id=1, source_target_pairs={{0,16},{16,32},{32,48},{48,64},{64,80},{80,96},{96,112},{112,128},... | collective-permute-start | bytes 245768 | tf_op jit(solution)/shard_map/ppermute | solution.py:19
  35.6 5.0 %collective-permute-start.6 = (f32[1,1,1,24,4]{4,3,2,1,0:T(8,128)S(1)}, f32[1,1,1,24,4]{4,3,2,1,0:T(8,128)S(1)}, u32[]{:S(2)}, u32[]{:S(2)}) collective-permute-start(f32[1,1,1,24,4]{4,3,2,1,0:T(8,128)S(1)} %get-tuple-element.72), channel_id=1, source_target_pairs={{0,2},{2,4},{4,6},{6,8},{8,10},{10,12},{12,14},{1,3},{3,5},{5,7},{... | collective-permute-start | bytes 1160 | tf_op jit(solution)/shard_map/ppermute | solution.py:19
  39.1 6.0 %collective-permute-start.7 = (f32[1,1,1,24,4]{4,3,2,1,0:T(8,128)S(1)}, f32[1,1,1,24,4]{4,3,2,1,0:T(8,128)S(1)}, u32[]{:S(2)}, u32[]{:S(2)}) collective-permute-start(f32[1,1,1,24,4]{4,3,2,1,0:T(8,128)S(1)} %get-tuple-element.73), channel_id=1, source_target_pairs={{2,0},{4,2},{6,4},{8,6},{10,8},{12,10},{14,12},{3,1},{5,3},{7,5},{... | collective-permute-start | bytes 1160 | tf_op jit(solution)/shard_map/ppermute | solution.py:21
  40.5 6.0 %collective-permute-start.10 = (f32[1,1,1,24,4]{4,3,2,1,0:T(8,128)S(1)}, f32[1,1,1,24,4]{4,3,2,1,0:T(8,128)S(1)}, u32[]{:S(2)}, u32[]{:S(2)}) collective-permute-start(f32[1,1,1,24,4]{4,3,2,1,0:T(8,128)S(1)} %get-tuple-element.70), channel_id=1, source_target_pairs={{0,2},{2,4},{4,6},{6,8},{8,10},{10,12},{12,14},{1,3},{3,5},{5,7},{... | collective-permute-start | bytes 1160 | tf_op jit(solution)/shard_map/ppermute | solution.py:19
  45.1 5.6 %collective-permute-start.11 = (f32[1,1,1,24,4]{4,3,2,1,0:T(8,128)S(1)}, f32[1,1,1,24,4]{4,3,2,1,0:T(8,128)S(1)}, u32[]{:S(2)}, u32[]{:S(2)}) collective-permute-start(f32[1,1,1,24,4]{4,3,2,1,0:T(8,128)S(1)} %get-tuple-element.71), channel_id=1, source_target_pairs={{2,0},{4,2},{6,4},{8,6},{10,8},{12,10},{14,12},{3,1},{5,3},{7,5},{... | collective-permute-start | bytes 1160 | tf_op jit(solution)/shard_map/ppermute | solution.py:21
  46.5 16.1 %collective-permute-start.1 = (f32[2,2,10,4,128]{4,3,2,1,0:T(4,128)S(1)}, f32[2,2,10,4,128]{4,3,2,1,0:T(4,128)S(1)}, u32[]{:S(2)}, u32[]{:S(2)}) collective-permute-start(f32[2,2,10,4,128]{4,3,2,1,0:T(4,128)S(1)} %get-tuple-element.61), channel_id=1, source_target_pairs={{16,0},{32,16},{48,32},{64,48},{80,64},{96,80},{112,96},{128,112},... | collective-permute-start | bytes 245768 | tf_op jit(solution)/shard_map/ppermute | solution.py:21
  51.1 5.5 %collective-permute-start.14 = (f32[2,1,1,24,4]{4,3,0,2,1:T(8,128)S(1)}, f32[2,1,1,24,4]{4,3,0,2,1:T(8,128)S(1)}, u32[]{:S(2)}, u32[]{:S(2)}) collective-permute-start(f32[2,1,1,24,4]{4,3,0,2,1:T(8,128)S(1)} %get-tuple-element.66), channel_id=1, source_target_pairs={{0,2},{2,4},{4,6},{6,8},{8,10},{10,12},{12,14},{1,3},{3,5},{5,7},{... | collective-permute-start | bytes 2312 | tf_op jit(solution)/shard_map/ppermute | solution.py:19
  55.1 7.0 %collective-permute-start.15 = (f32[2,1,1,24,4]{4,3,0,2,1:T(8,128)S(1)}, f32[2,1,1,24,4]{4,3,0,2,1:T(8,128)S(1)}, u32[]{:S(2)}, u32[]{:S(2)}) collective-permute-start(f32[2,1,1,24,4]{4,3,0,2,1:T(8,128)S(1)} %get-tuple-element.67), channel_id=1, source_target_pairs={{2,0},{4,2},{6,4},{8,6},{10,8},{12,10},{14,12},{3,1},{5,3},{7,5},{... | collective-permute-start | bytes 2312 | tf_op jit(solution)/shard_map/ppermute | solution.py:21
  62.2 1.0 copy-start
  63.5 11.5 %collective-permute-start.2 = (f32[2,2,10,24,4]{4,3,2,1,0:T(8,128)S(1)}, f32[2,2,10,24,4]{4,3,2,1,0:T(8,128)S(1)}, u32[]{:S(2)}, u32[]{:S(2)}) collective-permute-start(f32[2,2,10,24,4]{4,3,2,1,0:T(8,128)S(1)} %get-tuple-element.58), channel_id=1, source_target_pairs={{0,2},{2,4},{4,6},{6,8},{8,10},{10,12},{12,14},{1,3},{3,5},{5,7},{... | collective-permute-start | bytes 46088 | tf_op jit(solution)/shard_map/ppermute | solution.py:19
  68.7 10.8 %collective-permute-start.3 = (f32[2,2,10,24,4]{4,3,2,1,0:T(8,128)S(1)}, f32[2,2,10,24,4]{4,3,2,1,0:T(8,128)S(1)}, u32[]{:S(2)}, u32[]{:S(2)}) collective-permute-start(f32[2,2,10,24,4]{4,3,2,1,0:T(8,128)S(1)} %get-tuple-element.59), channel_id=1, source_target_pairs={{2,0},{4,2},{6,4},{8,6},{10,8},{12,10},{14,12},{3,1},{5,3},{7,5},{... | collective-permute-start | bytes 46088 | tf_op jit(solution)/shard_map/ppermute | solution.py:21
  91.3 0.7 copy-start.2
  91.3 0.7 copy-start.3
  91.3 0.7 copy-start.4
  91.3 0.7 copy-start.5
  100.9 5.9 %copy-start.1 = (f32[2,10,16,128]{3,2,1,0:T(8,128)S(1)}, f32[2,10,16,128]{3,2,1,0:T(8,128)}, u32[]{:S(2)}) copy-start(f32[2,10,16,128]{3,2,1,0:T(8,128)} %slice_bitcast_fusion.8) | copy-start | bytes 491524
where the time goes:
time: 189 us; the launch traced here: 187 us
  blocking collectives  77.5 us (41%)
  starting transfers between devices  55.2 us (29%)
  other arithmetic  31.8 us (17%)
  waiting for transfers between devices  17.7 us (9%)
  local copies, waits for them, and re-layouts  4.53 us (2%)
    psum x2, blocking collectives, one_axis_at_a_time(): value = lax.psum(value, axis)  75.4 us
    ppermute x8, starting transfers between devices, extended_2(): lax.ppermute(tail, axis, [(i, (i + 1) % count) for i in range(ends)])  44.6 us
    mul x3, other arithmetic, apply_local(): product = roots_wide * field_wide  15.1 us
    ppermute x8, waiting for transfers between devices, extended_2(): lax.ppermute(head, axis, [((i + 1) % count, i) for i in range(ends)])  12.8 us
    ppermute x8, starting transfers between devices, extended_2(): lax.ppermute(head, axis, [((i + 1) % count, i) for i in range(ends)])  10.6 us
    mul x2, other arithmetic, neighbour_sum(): addend = coefficient((step_z, step_x, step_y)) * window  7.57 us
    ppermute x8, waiting for transfers between devices, extended_2(): lax.ppermute(tail, axis, [(i, (i + 1) % count) for i in range(ends)])  4.88 us
  transfers between devices with their start and end apart: 16, of which 5 were waited for; matrix products, arithmetic and copies ran while one was open for 3% of the time, Pallas kernels for 0%

commit v1 on v0

v1 whole, which is shorter than its diff:
```python
import functools

import jax
import jax.numpy as jnp
from jax import lax
from jax.experimental import pallas as pl
from jax.experimental.pallas import tpu as pltpu
from jax.sharding import PartitionSpec as P

bed_unit = 2.0 ** (-29)
HALO = 4
TOP = 8
OWN = TOP + HALO
PITCH = 8
MESH = pl.DeviceIdType.MESH
along_z = 0.5
along_x = (0.25, 0.125)
along_y = (0.125, 0.25)
BED, MASK, FRICTION = 4, 5, 6
EDGE_U, EDGE_R, EDGE_0, EDGE_1, EDGE_2 = 0, 2, 3, 5, 7


def kernel(
    sizes,
    u_hbm,
    picks,
    table_hbm,
    bed_hbm,
    mask_hbm,
    out,
    uw,
    mw,
    xo,
    xl,
    xr,
    table,
    bed_in,
    mask_in,
    strip,
    shifted,
    edge,
    fixed,
    roots,
    tr,
    tp,
    tq,
    field_a,
    all_residual,
    all_image,
    all_start,
    gram,
    ring_y,
    ring_x,
    local_sem,
    halo_send,
    halo_recv,
    hand_sem,
    pair_send,
    pair_recv,
    y_send,
    y_recv,
    x_send,
    x_recv,
):
    planes, planeys = sizes
    members, comps, layers, rows, cols = u_hbm.shape
    wide = rows + 2 * HALO
    end = TOP + wide
    plane = lax.axis_index("plane")
    planey = lax.axis_index("planey")
    ens = lax.axis_index("ens")

    def at(dx, dy):
        return {
            "plane": lax.rem(plane + dx + planes, planes),
            "planey": lax.rem(planey + dy + planeys, planeys),
        }

    partner = {"ens": 1 - ens}
    around = [(dx, dy) for dx in (-1, 0, 1) for dy in (-1, 0, 1) if (dx, dy) != (0, 0)]

    def exists(dx, dy):
        flag = None
        for step, index, count in ((dx, plane, planes), (dy, planey, planeys)):
            if step != 0:
                part = index > 0 if step < 0 else index < count - 1
                flag = part if flag is None else jnp.logical_and(flag, part)
        return flag

    barrier = pltpu.get_barrier_semaphore()
    for dx, dy in around:
        pl.semaphore_signal(barrier, inc=1, device_id=at(dx, dy), device_id_type=MESH)
    pl.semaphore_signal(barrier, inc=1, device_id=partner, device_id_type=MESH)

    load_u = pltpu.make_async_copy(
        u_hbm, uw.at[:, :, pl.ds(1, layers), pl.ds(OWN, rows), :], local_sem.at[0]
    )
    load_table = pltpu.make_async_copy(table_hbm, table, local_sem.at[1])
    load_bed = pltpu.make_async_copy(bed_hbm, bed_in, local_sem.at[2])
    load_mask = pltpu.make_async_copy(mask_hbm, mask_in, local_sem.at[3])
    for load in (load_u, load_bed, load_mask, load_table):
        load.start()

    for end_layer in (0, layers + 1):
        uw[:, :, end_layer, TOP:end, :] = jnp.zeros((members, comps, wide, cols), jnp.float32)
        for buffer in (tr, tp, tq):
            buffer[:, end_layer] = jnp.zeros(buffer.shape[:1] + buffer.shape[2:], jnp.float32)
    for step, first in ((-1, TOP), (1, OWN + rows)):

        @pl.when(jnp.logical_not(exists(step, 0)))
        def _():
            uw[:, :, 1 : 1 + layers, first : first + HALO, :] = jnp.zeros(
                (members, comps, layers, HALO, cols), jnp.float32
            )
            for buffer in (mw, xo, xl, xr):
                buffer[:, first : first + HALO, :] = jnp.zeros(
                    (buffer.shape[0], HALO, cols), jnp.float32
                )

    for step, buffer in ((-1, xl), (1, xr)):

        @pl.when(jnp.logical_not(exists(0, step)))
        def _():
            buffer[:, TOP:end, :] = jnp.zeros((buffer.shape[0], wide, cols), jnp.float32)

    sends = []

    def send(number, dx, dy, source, target):
        copy = pltpu.make_async_remote_copy(
            src_ref=source,
            dst_ref=target,
            send_sem=halo_send.at[number],
            recv_sem=halo_recv.at[number],
            device_id=at(dx, dy),
            device_id_type=MESH,
        )

        @pl.when(exists(dx, dy))
        def _():
            copy.start()

        sends.append((copy, exists(dx, dy), exists(-dx, -dy)))

    def row_range(dx):
        if dx < 0:
            return pl.ds(OWN, HALO), pl.ds(OWN + rows, HALO)
        if dx > 0:
            return pl.ds(OWN + rows - HALO, HALO), pl.ds(TOP, HALO)
        return pl.ds(OWN, rows), pl.ds(OWN, rows)

    load_u.wait()
    pl.semaphore_wait(barrier, len(around) + 1)
    body = pl.ds(1, layers)
    for dx in (-1, 1):
        here, there = row_range(dx)
        send(
            0 if dx < 0 else 1,
            dx,
            0,
            uw.at[:, :, body, here, :],
            uw.at[:, :, body, there, :],
        )

    hands = []
    for axis, count in (("plane", planes), ("planey", planeys)):
        reach = 1
        while reach * 2 <= count // 2:
            hands.append((reach, axis))
            reach *= 2
    hands.sort()

    def greet(number):
        reach, axis = hands[number]
        for step in (-reach, reach):
            target = at(step, 0) if axis == "plane" else at(0, step)
            pl.semaphore_signal(
                hand_sem.at[number], inc=1, device_id=target, device_id_type=MESH
            )

    def greeted(number):
        pl.semaphore_wait(hand_sem.at[number], 2)

    def greet_round(reach):
        for number, (distance, _) in enumerate(hands):
            if distance == reach:
                greet(number)

    def greeted_round(reach):
        for number, (distance, _) in enumerate(hands):
            if distance == reach:
                greeted(number)

    greet_round(1)

    lane = lax.broadcasted_iota(jnp.int32, (rows, cols), 1)
    group = lane // PITCH
    load_bed.wait()
    load_mask.wait()
    load_table.wait()
    bed_own = bed_in[...].astype(jnp.float32) * bed_unit
    mask_own = mask_in[...].astype(jnp.float32)
    mw[0, OWN : OWN + rows, :] = bed_own
    mw[1, OWN : OWN + rows, :] = mask_own
    for member in range(members):
        chosen = table[picks[member]]
        mw[2 + member, OWN : OWN + rows, :] = chosen
        xo[FRICTION + member, OWN : OWN + rows, :] = jnp.where(
            lane < PITCH, pltpu.roll(chosen, HALO, 1), 0.0
        )
    for dx in (-1, 1):
        here, there = row_range(dx)
        send(2 if dx < 0 else 3, dx, 0, mw.at[:, here, :], mw.at[:, there, :])

    def lane_packed(planes_of):
        packed = jnp.zeros((rows, cols), jnp.float32)
        for layer in range(layers):
            turned = pltpu.roll(planes_of(layer), (PITCH * layer + HALO) % cols, 1)
            packed = jnp.where(group == layer, turned, packed)
        return packed

    xo[BED, OWN : OWN + rows, :] = lane_packed(lambda layer: bed_own)
    xo[MASK, OWN : OWN + rows, :] = lane_packed(lambda layer: mask_own)
    for member in range(members):
        for comp in range(comps):
            xo[member * comps + comp, OWN : OWN + rows, :] = lane_packed(
                lambda layer: uw[member, comp, 1 + layer, OWN : OWN + rows, :]
            )
    for number, (dx, dy) in enumerate(around):
        here, there = row_range(dx)
        target = xo if dy == 0 else (xr if dy < 0 else xl)
        send(4 + number, dx, dy, xo.at[:, here, :], target.at[:, there, :])

    greeted_round(1)
    greet_round(2)

    for copy, sent, arrives in sends:

        @pl.when(arrives)
        def _():
            copy.wait_recv()

    lane = lax.broadcasted_iota(jnp.int32, (wide, cols), 1)
    first_lane = lane == 0
    last_lane = lane == cols - 1
    spot = lax.rem(lane, PITCH)
    outer_left = spot < HALO
    left_edge = spot == HALO - 1
    position = (
        plane * rows - HALO + lax.broadcasted_iota(jnp.int32, (wide, cols), 0)
    ).astype(jnp.float32)
    thickness = 1.0 + 2.0 * position / (rows * planes - 1)

    def sides(number, low=TOP, high=end):
        own = xo[number, low:high, :]
        return (
            jnp.where(outer_left, xl[number, low:high, :], own),
            jnp.where(outer_left, own, xr[number, low:high, :]),
        )

    def edges(pair):
        left, right = pair
        return jnp.where(
            left_edge, pltpu.roll(right, cols - 1, 1), pltpu.roll(left, 1, 1)
        )

    def y_pair(value, near):
        return (
            jnp.where(last_lane, near, pltpu.roll(value, cols - 1, 1)),
            jnp.where(first_lane, near, pltpu.roll(value, 1, 1)),
        )

    def turned_edge(value, layer):
        return pltpu.roll(value, cols - HALO - PITCH * layer, 1)

    mask_main = mw[1, TOP:end, :]
    bed_plus, bed_minus = y_pair(mw[0, TOP:end, :], turned_edge(edges(sides(BED)), 0))
    scale = -(mask_main * thickness)
    fixed[0] = mask_main
    fixed[1] = scale * ((mw[0, TOP + 1 : end + 1, :] - mw[0, TOP - 1 : end - 1, :]) * 0.5)
    fixed[2] = scale * ((bed_plus - bed_minus) * 0.5)
    strip_force = []
    for side, (bed_here, mask_here) in enumerate(zip(sides(BED), sides(MASK))):
        shifted[side, TOP:end, :] = bed_here
        down = shifted[side, TOP + 1 : end + 1, :] - shifted[side, TOP - 1 : end - 1, :]
        flat = pltpu.roll(bed_here, cols - 1, 1) - pltpu.roll(bed_here, 1, 1)
        scale = -(mask_here * thickness)
        fixed[3 + side] = mask_here
        fixed[5 + side] = scale * (down * 0.5)
        fixed[7 + side] = scale * (flat * 0.5)

    def power(strain4):
        return jnp.exp(jnp.log(strain4 * 0.25 + 0.1) * (-1.0 / 6.0))

    def strain4_of(ui, vi, uj, vj, uz, vz):
        shear = uj + vi
        return ui * ui + vj * vj + ui * vj + 0.25 * (shear * shear + (uz * uz + vz * vz))

    def strip_k(pair, comp, slot):
        result = []
        for side, value in enumerate(pair):
            value = value + along_y[comp] * (
                pltpu.roll(value, cols - 1, 1) + pltpu.roll(value, 1, 1)
            )
            value = value + along_z * (
                pltpu.roll(value, cols - PITCH, 1) + pltpu.roll(value, PITCH, 1)
            )
            shifted[slot + side, TOP:end, :] = value
            result.append(
                value
                + along_x[comp]
                * (
                    shifted[slot + side, TOP + 1 : end + 1, :]
                    + shifted[slot + side, TOP - 1 : end - 1, :]
                )
            )
        return result

    own_top = lax.broadcasted_iota(jnp.int32, (8, cols), 0) >= HALO

    def own_sum(value):
        total = jnp.where(own_top, value[:8], value[wide - 8 :])
        for low in range(8, wide - 8, 8):
            total = total + value[low : low + 8]
        return total

    def sample(member, carry):
        base = member * comps
        for comp in range(comps):
            pair = sides(base + comp)
            edge[EDGE_U + comp] = edges(pair)
            for side in range(2):
                strip[comp * 2 + side, TOP:end, :] = pair[side]
        strip_roots = []
        strip_diag = []
        friction_pair = sides(FRICTION + member)
        for side in range(2):
            value = [strip[comp * 2 + side, TOP:end, :] for comp in range(comps)]
            step_i = [
                strip[comp * 2 + side, TOP + 1 : end + 1, :]
                - strip[comp * 2 + side, TOP - 1 : end - 1, :]
                for comp in range(comps)
            ]
            step_j = [pltpu.roll(v, cols - 1, 1) - pltpu.roll(v, 1, 1) for v in value]
            step_z = [pltpu.roll(v, cols - PITCH, 1) - pltpu.roll(v, PITCH, 1) for v in value]
            here = fixed[3 + side]
            strip_roots.append(
                here
                * power(
                    strain4_of(
                        step_i[0], step_i[1], step_j[0], step_j[1], step_z[0], step_z[1]
                    )
                )
            )
            strip_diag.append(here * friction_pair[side] + (1.0 - here))
        edge[EDGE_R] = edges(strip_roots)
        for comp in range(comps):
            around_roots = strip_k(strip_roots, comp, comp * 2)
            start = [
                fixed[3 + side] * strip[comp * 2 + side, TOP:end, :] for side in range(2)
            ]
            field = [strip_roots[side] * start[side] for side in range(2)]
            edge[EDGE_0 + comp] = edges(field)
            near = strip_k(field, comp, comp * 2)
            four = [4.0 * strip_roots[side] for side in range(2)]
            main = [
                four[side] * around_roots[side] + strip_diag[side] for side in range(2)
            ]
            residual = [
                fixed[5 + 2 * comp + side]
                - (main[side] * start[side] - four[side] * near[side])
                for side in range(2)
            ]
            field = [strip_roots[side] * residual[side] for side in range(2)]
            edge[EDGE_1 + comp] = edges(field)
            near = strip_k(field, comp, comp * 2)
            image = [
                main[side] * residual[side] - four[side] * near[side] for side in range(2)
            ]
            edge[EDGE_2 + comp] = edges([strip_roots[side] * image[side] for side in range(2)])

        def roots_and_start(layer, carry):
            here = fixed[0]
            value = [uw[member, comp, layer + 1, TOP:end, :] for comp in range(comps)]
            step_i = [
                uw[member, comp, layer + 1, TOP + 1 : end + 1, :]
                - uw[member, comp, layer + 1, TOP - 1 : end - 1, :]
                for comp in range(comps)
            ]
            step_j = []
            for comp in range(comps):
                plus, minus = y_pair(value[comp], turned_edge(edge[EDGE_U + comp], layer))
                step_j.append(plus - minus)
            step_z = [
                uw[member, comp, layer + 2, TOP:end, :] - uw[member, comp, layer, TOP:end, :]
                for comp in range(comps)
            ]
            root = here * power(
                strain4_of(step_i[0], step_i[1], step_j[0], step_j[1], step_z[0], step_z[1])
            )
            roots[layer] = root
            plus, minus = y_pair(root, turned_edge(edge[EDGE_R], layer))
            both = plus + minus
            for comp in range(comps):
                tr[comp, layer + 1, TOP:end, :] = root + along_y[comp] * both
                field = root * (here * value[comp])
                plus, minus = y_pair(field, turned_edge(edge[EDGE_0 + comp], layer))
                tp[comp, layer + 1, TOP:end, :] = field + along_y[comp] * (plus + minus)
            return carry

        def x_sum(buffer, comp, layer):
            return buffer[comp, layer, TOP:end, :] + along_x[comp] * (
                buffer[comp, layer, TOP + 1 : end + 1, :]
                + buffer[comp, layer, TOP - 1 : end - 1, :]
            )

        lax.fori_loop(0, layers, roots_and_start, 0, unroll=UNROLL)
        slot = members * ens + member
        empty = jnp.zeros((wide, cols), jnp.float32)

        def residual_layer(layer, carry):
            before, now, total = carry
            root = roots[layer]
            four = 4.0 * root
            here = fixed[0]
            bottom = jnp.where(layer == 0, 1.0, 0.0)
            diag = here * mw[2 + member, TOP:end, :] * bottom + (1.0 - here)
            after = []
            for comp in range(comps):
                after_r = x_sum(tr, comp, layer + 2)
                after_p = x_sum(tp, comp, layer + 2)
                after += [after_r, after_p]
                around_roots = now[2 * comp] + along_z * (before[2 * comp] + after_r)
                near = now[2 * comp + 1] + along_z * (before[2 * comp + 1] + after_p)
                main = four * around_roots + diag
                start = here * uw[member, comp, layer + 1, TOP:end, :]
                residual = fixed[1 + comp] - (main * start - four * near)
                field_a[comp, layer] = main
                all_residual[slot, comp, layer] = residual
                total = total + own_sum(residual * residual)
                field = root * residual
                plus, minus = y_pair(field, turned_edge(edge[EDGE_1 + comp], layer))
                tq[comp, layer + 1, TOP:end, :] = field + along_y[comp] * (plus + minus)
            return tuple(now), tuple(after), total

        nothing = jnp.zeros((8, cols), jnp.float32)
        first = tuple(
            x_sum(buffer, comp, 1) for comp in range(comps) for buffer in (tr, tp)
        )
        _, _, gram_rr = lax.fori_loop(
            0, layers, residual_layer, ((empty,) * 4, first, nothing), unroll=UNROLL
        )

        def image_layer(layer, carry):
            before, now, total_ra, total_aa = carry
            root = roots[layer]
            four = 4.0 * root
            after = []
            for comp in range(comps):
                after_p = x_sum(tq, comp, layer + 2)
                after.append(after_p)
                near = now[comp] + along_z * (before[comp] + after_p)
                residual = all_residual[slot, comp, layer]
                image = field_a[comp, layer] * residual - four * near
                all_image[slot, comp, layer] = image
                total_ra = total_ra + own_sum(residual * image)
                total_aa = total_aa + own_sum(image * image)
                field = root * image
                plus, minus = y_pair(field, turned_edge(edge[EDGE_2 + comp], layer))
                tp[comp, layer + 1, TOP:end, :] = field + along_y[comp] * (plus + minus)
            return tuple(now), tuple(after), total_ra, total_aa

        first = tuple(x_sum(tq, comp, 1) for comp in range(comps))
        _, _, gram_ra, gram_aa = lax.fori_loop(
            0,
            layers,
            image_layer,
            ((empty,) * 2, first, nothing, nothing),
            unroll=UNROLL,
        )

        def own_x_sum(comp, layer):
            return tp[comp, layer, OWN : OWN + rows, :] + along_x[comp] * (
                tp[comp, layer, OWN + 1 : OWN + rows + 1, :]
                + tp[comp, layer, OWN - 1 : OWN + rows - 1, :]
            )

        def second_layer(layer, carry):
            before, now, total = carry
            four = 4.0 * roots[layer, HALO : HALO + rows, :]
            after = []
            for comp in range(comps):
                after_p = own_x_sum(comp, layer + 2)
                after.append(after_p)
                near = now[comp] + along_z * (before[comp] + after_p)
                image = all_image[slot, comp, layer, HALO : HALO + rows, :]
                second = (
                    field_a[comp, layer, HALO : HALO + rows, :] * image - four * near
                )
                product = image * second
                for low in range(0, rows, 8):
                    total = total + product[low : low + 8]
            return tuple(now), tuple(after), total

        empty_own = jnp.zeros((rows, cols), jnp.float32)
        first = tuple(own_x_sum(comp, 1) for comp in range(comps))
        _, _, gram_ab = lax.fori_loop(
            0, layers, second_layer, ((empty_own,) * 2, first, nothing), unroll=UNROLL
        )
        for number, value in enumerate((gram_rr, gram_ra, gram_aa, gram_ab)):
            gram[4 * member + number] = value
        return carry

    greeted_round(2)
    greet_round(4)
    lax.fori_loop(0, members, sample, 0)
    for reach in (4, 8, 16):
        greeted_round(reach)
        if reach > 2:
            greet_round(2 * reach)
    pl.semaphore_signal(
        hand_sem.at[len(hands)], inc=1, device_id=partner, device_id_type=MESH
    )

    lines = 4 * members
    total = jnp.sum(gram[...], axis=1)
    total = jnp.sum(total, axis=1, keepdims=True)
    lane = lax.broadcasted_iota(jnp.int32, (lines, cols), 1)
    line = lax.broadcasted_iota(jnp.int32, (lines, cols), 0)
    message = jnp.sum(
        jnp.where(lane == line + lines * ens, total, 0.0), axis=0, keepdims=True
    )
    pl.semaphore_wait(hand_sem.at[len(hands)], 1)

    def exchange(ring, me, count, target, send_sem, recv_sem, value):
        ring[me] = value
        copies = []
        for offset in range(1, count):
            copy = pltpu.make_async_remote_copy(
                src_ref=ring.at[me],
                dst_ref=ring.at[me],
                send_sem=send_sem.at[offset],
                recv_sem=recv_sem.at[offset],
                device_id=target(lax.rem(me + offset, count)),
                device_id_type=MESH,
            )
            copy.start()
            copies.append(copy)
        return copies

    cores = 2
    copies_y = exchange(
        ring_y,
        planey * cores + ens,
        planeys * cores,
        lambda peer: {"planey": peer // cores, "ens": lax.rem(peer, cores)},
        y_send,
        y_recv,
        message,
    )

    mine = pl.ds(members * ens, members)
    inner = pl.ds(HALO, rows)
    fields = []
    for comp in range(comps):
        for layer in range(layers):
            total = None
            for member in range(members):
                start = mw[1, OWN : OWN + rows, :] * uw[member, comp, layer + 1, OWN : OWN + rows, :]
                total = start if total is None else total + start
            all_start[ens, comp, layer] = total
    for number, (source, target) in enumerate(
        (
            (all_residual.at[mine, :, :, inner, :],) * 2,
            (all_image.at[mine, :, :, inner, :],) * 2,
            (all_start.at[ens],) * 2,
        )
    ):
        copy = pltpu.make_async_remote_copy(
            src_ref=source,
            dst_ref=target,
            send_sem=pair_send.at[number],
            recv_sem=pair_recv.at[number],
            device_id=partner,
            device_id_type=MESH,
        )
        copy.start()
        fields.append(copy)

    for copy in copies_y:
        copy.wait_recv()
    copies_x = exchange(
        ring_x,
        plane,
        planes,
        lambda peer: {"plane": peer},
        x_send,
        x_recv,
        jnp.sum(ring_y[...], axis=0),
    )
    for copy in fields:
        copy.wait_recv()
    for copy in copies_x:
        copy.wait_recv()
    sums = jnp.sum(ring_x[...], axis=0)
    gram_rr = sums
    gram_ra = pltpu.roll(sums, cols - 1, 1)
    gram_aa = pltpu.roll(sums, cols - 2, 1)
    gram_ab = pltpu.roll(sums, cols - 3, 1)
    first_step = gram_rr / gram_ra
    norm_next = gram_rr - 2.0 * first_step * gram_ra + first_step * first_step * gram_aa
    growth = 1.0 + norm_next / gram_rr
    curve = (
        growth * growth * gram_ra
        - 2.0 * growth * first_step * gram_aa
        + first_step * first_step * gram_ab
    )
    second_step = norm_next / curve
    samples = members * cores
    share = 1.0 / samples
    for_residual = share * (first_step + second_step * growth)
    for_image = share * (second_step * first_step)
    lane = lax.broadcasted_iota(jnp.int32, (1, cols), 1)

    def pick(value, number):
        return jnp.sum(jnp.where(lane == 4 * number, value, 0.0), axis=1, keepdims=True)

    weights = [(pick(for_residual, k), pick(for_image, k)) for k in range(samples)]

    def combine(layer, carry):
        for comp in range(comps):
            total = share * (all_start[0, comp, layer] + all_start[1, comp, layer])
            for number in range(samples):
                total = total + (
                    weights[number][0] * all_residual[number, comp, layer, HALO : HALO + rows, :]
                    - weights[number][1] * all_image[number, comp, layer, HALO : HALO + rows, :]
                )
            out[comp, layer] = total
        return carry

    lax.fori_loop(0, layers, combine, 0, unroll=UNROLL)

    for copy, sent, arrives in sends:

        @pl.when(sent)
        def _():
            copy.wait_send()

    for copy in copies_y + fields + copies_x:
        copy.wait_send()


UNROLL = 2


def body(sizes, u_prior, friction_rows, friction_table, bed_fixed, ice_mask):
    planes, planeys = sizes
    members, comps, layers, rows, cols = u_prior.shape
    wide = rows + 2 * HALO
    deep = rows + 24
    samples = 2 * members
    f32 = jnp.float32
    anywhere = pl.BlockSpec(memory_space=pl.ANY)
    fields = FRICTION + members
    vmem = pltpu.VMEM
    dma = pltpu.SemaphoreType.DMA
    return pl.pallas_call(
        functools.partial(kernel, sizes),
        out_shape=jax.ShapeDtypeStruct((comps, layers, rows, cols), f32),
        in_specs=[
            anywhere,
            pl.BlockSpec(memory_space=pltpu.SMEM),
            anywhere,
            anywhere,
            anywhere,
        ],
        out_specs=pl.BlockSpec(memory_space=pltpu.VMEM),
        scratch_shapes=[
            vmem((members, comps, layers + 2, deep, cols), f32),
            vmem((2 + members, deep, cols), f32),
            vmem((fields, deep, cols), f32),
            vmem((fields, deep, cols), f32),
            vmem((fields, deep, cols), f32),
            vmem(friction_table.shape, f32),
            vmem((rows, cols), jnp.int32),
            vmem((rows, cols), jnp.int32),
            vmem((2 * comps, deep, cols), f32),
            vmem((2 * comps, deep, cols), f32),
            vmem((9, wide, cols), f32),
            vmem((9, wide, cols), f32),
            vmem((layers, wide, cols), f32),
            vmem((comps, layers + 2, deep, cols), f32),
            vmem((comps, layers + 2, deep, cols), f32),
            vmem((comps, layers + 2, deep, cols), f32),
            vmem((comps, layers, wide, cols), f32),
            vmem((samples, comps, layers, wide, cols), f32),
            vmem((samples, comps, layers, wide, cols), f32),
            vmem((2, comps, layers, rows, cols), f32),
            vmem((4 * members, 8, cols), f32),
            vmem((2 * planeys, 1, cols), f32),
            vmem((planes, 1, cols), f32),
            dma((4,)),
            dma((12,)),
            dma((12,)),
            pltpu.SemaphoreType.REGULAR((8,)),
            dma((3,)),
            dma((3,)),
            dma((2 * planeys,)),
            dma((2 * planeys,)),
            dma((planes,)),
            dma((planes,)),
        ],
        compiler_params=pltpu.CompilerParams(
            collective_id=0, has_side_effects=True, vmem_limit_bytes=48 * 1024 * 1024
        ),
    )(u_prior, friction_rows, friction_table, bed_fixed, ice_mask)


def solution(mesh):
    in_specs = (
        P(("group", "ens"), None, None, "plane", "planey"),
        P(("group", "ens")),
        P("group", "plane", "planey"),
        P("plane", "planey"),
        P("plane", "planey"),
    )
    out_specs = P("group", None, "plane", "planey")
    sizes = (mesh.shape["plane"], mesh.shape["planey"])
    return jax.shard_map(
        functools.partial(body, sizes),
        mesh=mesh,
        in_specs=in_specs,
        out_specs=out_specs,
        check_vma=False,
    )
```

time: 189 us -> 74 us (0.39)
  blocking collectives: 77.5 us -> 0 us
  Pallas kernels: 0 us -> 69.2 us
  starting transfers between devices: 55.2 us -> 0 us
  other arithmetic: 31.8 us -> 0 us
  waiting for transfers between devices: 17.7 us -> 0 us
    psum x2 -> x0, blocking collectives: 75.4 us -> none  [one_axis_at_a_time(): value = lax.psum(value, axis)]
    pallas_call x0 -> x1, Pallas kernels: none -> 69.2 us  [body(): pl.pallas_call(functools.partial(kernel, sizes), out_shape=jax.ShapeDtype...]
    ppermute x16 -> x0, starting transfers between devices: 55.2 us -> none  [the longest x8 44.6 us: extended_2(): lax.ppermute(tail, axis, [(i, (i + 1) % count) for i in range(ends)])]
    mul x9 -> x0, other arithmetic: 24.6 us -> none  [the longest x3 15.1 us: apply_local(): product = roots_wide * field_wide]
    ppermute x16 -> x0, waiting for transfers between devices: 17.7 us -> none  [the longest x8 12.8 us: extended_2(): lax.ppermute(head, axis, [((i + 1) % count, i) for i in range(ends)])]
    unnamed x12 -> x11, local copies, waits for them, and re-layouts: 0.87 us -> 4.59 us
    reduce_sum x4 -> x0, other arithmetic: 3.14 us -> none  [the longest x1 1.79 us: inner(): return jnp.sum(left * right, axis=(1, 2, 3, 4))]
    mul x5 -> x0, local copies, waits for them, and re-layouts: 2.2 us -> none  [the longest x2 1.82 us: apply_local(): trimmed(roots_wide, 1) * (across_part * centre - nearby)]
  transfers between devices with their start and end apart: 16 -> 0, of which waited for: 5 -> 0; matrix products, arithmetic and copies ran while one was open for 3% -> 0% of each run, Pallas kernels for 0% -> 0%
where the time goes in v1:
time: 74 us; the launch traced here: 73.8 us
  Pallas kernels  69.2 us (94%)
  local copies, waits for them, and re-layouts  4.59 us (6%)
    pallas_call x1, Pallas kernels, body(): pl.pallas_call(functools.partial(kernel, sizes), out_shape=jax.ShapeDtype...  69.2 us
    unnamed x11, local copies, waits for them, and re-layouts  4.59 us

profile of v1, /device:TPU:80, one launch (start us, length us, event | category | flops | bytes accessed | tf_op | source)
XLA Modules:
  0.0 73.8 jit_solution(11297639361558141711)
XLA Ops:
  0.0 0.0 copy-start
  0.0 1.0 %copy-done = f32[2,2,10,16,128]{4,3,2,1,0:T(8,128)S(1)} copy-done((f32[2,2,10,16,128]{4,3,2,1,0:T(8,128)S(1)}, f32[2,2,10,16,128]{4,3,2,1,0:T(8,128)}, u32[]{:S(2)}) %copy-start) | copy-done | bytes 327704
  1.0 0.0 copy-start.1
  1.0 0.9 %copy-done.1 = f32[16,16,128]{2,1,0:T(8,128)S(1)} copy-done((f32[16,16,128]{2,1,0:T(8,128)S(1)}, f32[16,16,128]{2,1,0:T(8,128)}, u32[]{:S(2)}) %copy-start.1) | copy-done | bytes 131096
  1.9 0.0 copy-start.2
  1.9 0.7 copy-done.2
  2.6 0.0 copy-start.3
  2.6 0.7 copy-done.3
  3.3 0.0 copy-start.4
  3.3 0.7 copy-done.4
  3.9 69.2 %shard_map.55 = f32[2,10,16,128]{3,2,1,0:T(8,128)S(1)} custom-call(f32[2,2,10,16,128]{4,3,2,1,0:T(8,128)S(1)} %copy-done, s32[2]{0:T(128)S(1)} %copy-done.4, f32[16,16,128]{2,1,0:T(8,128)S(1)} %copy-done.1, s32[16,128]{1,0:T(8,128)S(1)} %copy-done.2, s32[16,128]{1,0:T(8,128)S(1)} %copy-done.3), custom_call_target="tpu_custom_call" | custom-call | tf_op jit(solution)/shard_map/pallas_call | solution.py:666
  73.1 0.7 copy.7
Async XLA Ops:
  0.0 1.0 %copy-start = (f32[2,2,10,16,128]{4,3,2,1,0:T(8,128)S(1)}, f32[2,2,10,16,128]{4,3,2,1,0:T(8,128)}, u32[]{:S(2)}) copy-start(f32[2,2,10,16,128]{4,3,2,1,0:T(8,128)} %u_hbm.1) | copy-start | bytes 983044
  1.0 0.9 %copy-start.1 = (f32[16,16,128]{2,1,0:T(8,128)S(1)}, f32[16,16,128]{2,1,0:T(8,128)}, u32[]{:S(2)}) copy-start(f32[16,16,128]{2,1,0:T(8,128)} %table_hbm.1) | copy-start | bytes 393220
  1.9 0.7 copy-start.2
  2.6 0.7 copy-start.3
  3.3 0.7 copy-start.4

commit v2 on v1

--- a/solution.py
+++ b/solution.py
@@ -1,3 +1,4 @@
+import contextlib
 import functools
 
 import jax
@@ -17,13 +18,20 @@
 along_x = (0.25, 0.125)
 along_y = (0.125, 0.25)
 BED, MASK, FRICTION = 4, 5, 6
+UNROLL = 10
+
+
+def scope(name):
+    return contextlib.nullcontext()
+
+
 EDGE_U, EDGE_R, EDGE_0, EDGE_1, EDGE_2 = 0, 2, 3, 5, 7
 
 
 def kernel(
     sizes,
     u_hbm,
-    picks,
+    picks_hbm,
     table_hbm,
     bed_hbm,
     mask_hbm,
@@ -36,6 +44,7 @@
     table,
     bed_in,
     mask_in,
+    picks,
     strip,
     shifted,
     edge,
@@ -98,7 +107,8 @@
     load_table = pltpu.make_async_copy(table_hbm, table, local_sem.at[1])
     load_bed = pltpu.make_async_copy(bed_hbm, bed_in, local_sem.at[2])
     load_mask = pltpu.make_async_copy(mask_hbm, mask_in, local_sem.at[3])
-    for load in (load_u, load_bed, load_mask, load_table):
+    load_picks = pltpu.make_async_copy(picks_hbm, picks, local_sem.at[4])
+    for load in (load_u, load_bed, load_mask, load_picks, load_table):
         load.start()
 
     for end_layer in (0, layers + 1):
@@ -148,8 +158,71 @@
             return pl.ds(OWN + rows - HALO, HALO), pl.ds(TOP, HALO)
         return pl.ds(OWN, rows), pl.ds(OWN, rows)
 
-    load_u.wait()
-    pl.semaphore_wait(barrier, len(around) + 1)
+    hands = []
+    for axis, count in (("plane", planes), ("planey", planeys)):
+        reach = 1
+        while reach * 2 <= count // 2:
+            hands.append((reach, axis))
+            reach *= 2
+    hands.sort()
+
+    def greet(number):
+        reach, axis = hands[number]
+        for step in (-reach, reach):
+            target = at(step, 0) if axis == "plane" else at(0, step)
+            pl.semaphore_signal(
+                hand_sem.at[number], inc=1, device_id=target, device_id_type=MESH
+            )
+
+    def greeted(number):
+        pl.semaphore_wait(hand_sem.at[number], 2)
+
+    def greet_round(reach):
+        for number, (distance, _) in enumerate(hands):
+            if distance == reach:
+                greet(number)
+
+    def greeted_round(reach):
+        for number, (distance, _) in enumerate(hands):
+            if distance == reach:
+                greeted(number)
+
+    with scope("p0_load"):
+        load_u.wait()
+        load_bed.wait()
+        load_mask.wait()
+        load_picks.wait()
+        load_table.wait()
+    lane = lax.broadcasted_iota(jnp.int32, (rows, cols), 1)
+    group = lane // PITCH
+    bed_own = bed_in[...].astype(jnp.float32) * bed_unit
+    mask_own = mask_in[...].astype(jnp.float32)
+    mw[0, OWN : OWN + rows, :] = bed_own
+    mw[1, OWN : OWN + rows, :] = mask_own
+    for member in range(members):
+        chosen = table[picks[member]]
+        mw[2 + member, OWN : OWN + rows, :] = chosen
+        xo[FRICTION + member, OWN : OWN + rows, :] = jnp.where(
+            lane < PITCH, pltpu.roll(chosen, HALO, 1), 0.0
+        )
+
+    def lane_packed(planes_of):
+        packed = jnp.zeros((rows, cols), jnp.float32)
+        for layer in range(layers):
+            turned = pltpu.roll(planes_of(layer), (PITCH * layer + HALO) % cols, 1)
+            packed = jnp.where(group == layer, turned, packed)
+        return packed
+
+    xo[BED, OWN : OWN + rows, :] = lane_packed(lambda layer: bed_own)
+    xo[MASK, OWN : OWN + rows, :] = lane_packed(lambda layer: mask_own)
+    for member in range(members):
+        for comp in range(comps):
+            xo[member * comps + comp, OWN : OWN + rows, :] = lane_packed(
+                lambda layer: uw[member, comp, 1 + layer, OWN : OWN + rows, :]
+            )
+
+    with scope("p1_barrier"):
+        pl.semaphore_wait(barrier, len(around) + 1)
     body = pl.ds(1, layers)
     for dx in (-1, 1):
         here, there = row_range(dx)
@@ -160,84 +233,25 @@
             uw.at[:, :, body, here, :],
             uw.at[:, :, body, there, :],
         )
-
-    hands = []
-    for axis, count in (("plane", planes), ("planey", planeys)):
-        reach = 1
-        while reach * 2 <= count // 2:
-            hands.append((reach, axis))
-            reach *= 2
-    hands.sort()
-
-    def greet(number):
-        reach, axis = hands[number]
-        for step in (-reach, reach):
-            target = at(step, 0) if axis == "plane" else at(0, step)
-            pl.semaphore_signal(
-                hand_sem.at[number], inc=1, device_id=target, device_id_type=MESH
-            )
-
-    def greeted(number):
-        pl.semaphore_wait(hand_sem.at[number], 2)
-
-    def greet_round(reach):
-        for number, (distance, _) in enumerate(hands):
-            if distance == reach:
-                greet(number)
-
-    def greeted_round(reach):
-        for number, (distance, _) in enumerate(hands):
-            if distance == reach:
-                greeted(number)
-
     greet_round(1)
-
-    lane = lax.broadcasted_iota(jnp.int32, (rows, cols), 1)
-    group = lane // PITCH
-    load_bed.wait()
-    load_mask.wait()
-    load_table.wait()
-    bed_own = bed_in[...].astype(jnp.float32) * bed_unit
-    mask_own = mask_in[...].astype(jnp.float32)
-    mw[0, OWN : OWN + rows, :] = bed_own
-    mw[1, OWN : OWN + rows, :] = mask_own
-    for member in range(members):
-        chosen = table[picks[member]]
-        mw[2 + member, OWN : OWN + rows, :] = chosen
-        xo[FRICTION + member, OWN : OWN + rows, :] = jnp.where(
-            lane < PITCH, pltpu.roll(chosen, HALO, 1), 0.0
-        )
-    for dx in (-1, 1):
-        here, there = row_range(dx)
-        send(2 if dx < 0 else 3, dx, 0, mw.at[:, here, :], mw.at[:, there, :])
-
-    def lane_packed(planes_of):
-        packed = jnp.zeros((rows, cols), jnp.float32)
-        for layer in range(layers):
-            turned = pltpu.roll(planes_of(layer), (PITCH * layer + HALO) % cols, 1)
-            packed = jnp.where(group == layer, turned, packed)
-        return packed
-
-    xo[BED, OWN : OWN + rows, :] = lane_packed(lambda layer: bed_own)
-    xo[MASK, OWN : OWN + rows, :] = lane_packed(lambda layer: mask_own)
-    for member in range(members):
-        for comp in range(comps):
-            xo[member * comps + comp, OWN : OWN + rows, :] = lane_packed(
-                lambda layer: uw[member, comp, 1 + layer, OWN : OWN + rows, :]
-            )
     for number, (dx, dy) in enumerate(around):
         here, there = row_range(dx)
         target = xo if dy == 0 else (xr if dy < 0 else xl)
         send(4 + number, dx, dy, xo.at[:, here, :], target.at[:, there, :])
-
-    greeted_round(1)
+    for dx in (-1, 1):
+        here, there = row_range(dx)
+        send(2 if dx < 0 else 3, dx, 0, mw.at[:, here, :], mw.at[:, there, :])
+
+    with scope("p3_greeted1"):
+        greeted_round(1)
     greet_round(2)
 
-    for copy, sent, arrives in sends:
-
-        @pl.when(arrives)
-        def _():
-            copy.wait_recv()
+    with scope("p4_halo"):
+        for copy, sent, arrives in sends:
+
+            @pl.when(arrives)
+            def _():
+                copy.wait_recv()
 
     lane = lax.broadcasted_iota(jnp.int32, (wide, cols), 1)
     first_lane = lane == 0
@@ -413,7 +427,8 @@
                 + buffer[comp, layer, TOP - 1 : end - 1, :]
             )
 
-        lax.fori_loop(0, layers, roots_and_start, 0, unroll=UNROLL)
+        with scope("q1_roots"):
+            lax.fori_loop(0, layers, roots_and_start, 0, unroll=UNROLL)
         slot = members * ens + member
         empty = jnp.zeros((wide, cols), jnp.float32)
 
@@ -446,9 +461,10 @@
         first = tuple(
             x_sum(buffer, comp, 1) for comp in range(comps) for buffer in (tr, tp)
         )
-        _, _, gram_rr = lax.fori_loop(
-            0, layers, residual_layer, ((empty,) * 4, first, nothing), unroll=UNROLL
-        )
+        with scope("q2_residual"):
+            _, _, gram_rr = lax.fori_loop(
+                0, layers, residual_layer, ((empty,) * 4, first, nothing), unroll=UNROLL
+            )
 
         def image_layer(layer, carry):
             before, now, total_ra, total_aa = carry
@@ -470,13 +486,14 @@
             return tuple(now), tuple(after), total_ra, total_aa
 
         first = tuple(x_sum(tq, comp, 1) for comp in range(comps))
-        _, _, gram_ra, gram_aa = lax.fori_loop(
-            0,
-            layers,
-            image_layer,
-            ((empty,) * 2, first, nothing, nothing),
-            unroll=UNROLL,
-        )
+        with scope("q3_image"):
+            _, _, gram_ra, gram_aa = lax.fori_loop(
+                0,
+                layers,
+                image_layer,
+                ((empty,) * 2, first, nothing, nothing),
+                unroll=UNROLL,
+            )
 
         def own_x_sum(comp, layer):
             return tp[comp, layer, OWN : OWN + rows, :] + along_x[comp] * (
@@ -503,23 +520,36 @@
 
         empty_own = jnp.zeros((rows, cols), jnp.float32)
         first = tuple(own_x_sum(comp, 1) for comp in range(comps))
-        _, _, gram_ab = lax.fori_loop(
-            0, layers, second_layer, ((empty_own,) * 2, first, nothing), unroll=UNROLL
-        )
+        with scope("q4_second"):
+            _, _, gram_ab = lax.fori_loop(
+                0, layers, second_layer, ((empty_own,) * 2, first, nothing), unroll=UNROLL
+            )
         for number, value in enumerate((gram_rr, gram_ra, gram_aa, gram_ab)):
             gram[4 * member + number] = value
         return carry
 
-    greeted_round(2)
+    with scope("p5_greeted2"):
+        greeted_round(2)
     greet_round(4)
-    lax.fori_loop(0, members, sample, 0)
-    for reach in (4, 8, 16):
-        greeted_round(reach)
-        if reach > 2:
-            greet_round(2 * reach)
-    pl.semaphore_signal(
-        hand_sem.at[len(hands)], inc=1, device_id=partner, device_id_type=MESH
-    )
+
+    def one_sample(member, carry):
+        sample(member, carry)
+
+        @pl.when(member == 0)
+        def _():
+            with scope("p6_greeted4"):
+                for reach in (4, 8, 16):
+                    greeted_round(reach)
+                    if reach > 2:
+                        greet_round(2 * reach)
+            pl.semaphore_signal(
+                hand_sem.at[len(hands)], inc=1, device_id=partner, device_id_type=MESH
+            )
+
+        return carry
+
+    with scope("p6_samples"):
+        lax.fori_loop(0, members, one_sample, 0)
 
     lines = 4 * members
     total = jnp.sum(gram[...], axis=1)
@@ -529,23 +559,28 @@
     message = jnp.sum(
         jnp.where(lane == line + lines * ens, total, 0.0), axis=0, keepdims=True
     )
-    pl.semaphore_wait(hand_sem.at[len(hands)], 1)
+    with scope("p7_hand"):
+        pl.semaphore_wait(hand_sem.at[len(hands)], 1)
 
     def exchange(ring, me, count, target, send_sem, recv_sem, value):
         ring[me] = value
-        copies = []
-        for offset in range(1, count):
-            copy = pltpu.make_async_remote_copy(
+        for offset in sorted(range(1, count), key=lambda k: -min(k, count - k)):
+            pltpu.make_async_remote_copy(
                 src_ref=ring.at[me],
                 dst_ref=ring.at[me],
-                send_sem=send_sem.at[offset],
-                recv_sem=recv_sem.at[offset],
+                send_sem=send_sem.at[0],
+                recv_sem=recv_sem.at[0],
                 device_id=target(lax.rem(me + offset, count)),
                 device_id_type=MESH,
-            )
-            copy.start()
-            copies.append(copy)
-        return copies
+            ).start()
+        return pltpu.make_async_remote_copy(
+            src_ref=ring.at[pl.ds(0, count - 1)],
+            dst_ref=ring.at[pl.ds(0, count - 1)],
+            send_sem=send_sem.at[0],
+            recv_sem=recv_sem.at[0],
+            device_id=target(lax.rem(me + 1, count)),
+            device_id_type=MESH,
+        )
 
     cores = 2
     copies_y = exchange(
@@ -586,8 +621,14 @@
         copy.start()
         fields.append(copy)
 
-    for copy in copies_y:
-        copy.wait_recv()
+    for copy, sent, arrives in sends:
+
+        @pl.when(sent)
+        def _():
+            copy.wait_send()
+
+    with scope("p8_ary"):
+        copies_y.wait_recv()
     copies_x = exchange(
         ring_x,
         plane,
@@ -599,8 +640,10 @@
     )
     for copy in fields:
         copy.wait_recv()
-    for copy in copies_x:
-        copy.wait_recv()
+    for copy in fields + [copies_y]:
+        copy.wait_send()
+    with scope("p9_arx"):
+        copies_x.wait_recv()
     sums = jnp.sum(ring_x[...], axis=0)
     gram_rr = sums
     gram_ra = pltpu.roll(sums, cols - 1, 1)
@@ -637,19 +680,10 @@
             out[comp, layer] = total
         return carry
 
-    lax.fori_loop(0, layers, combine, 0, unroll=UNROLL)
-
-    for copy, sent, arrives in sends:
-
-        @pl.when(sent)
-        def _():
-            copy.wait_send()
-
-    for copy in copies_y + fields + copies_x:
-        copy.wait_send()
-
-
-UNROLL = 2
+    with scope("pa_combine"):
+        lax.fori_loop(0, layers, combine, 0, unroll=UNROLL)
+    with scope("pb_sent"):
+        copies_x.wait_send()
 
 
 def body(sizes, u_prior, friction_rows, friction_table, bed_fixed, ice_mask):
@@ -659,20 +693,14 @@
     deep = rows + 24
     samples = 2 * members
     f32 = jnp.float32
-    anywhere = pl.BlockSpec(memory_space=pl.ANY)
+    anywhere = pl.BlockSpec(memory_space=pltpu.HBM)
     fields = FRICTION + members
     vmem = pltpu.VMEM
     dma = pltpu.SemaphoreType.DMA
     return pl.pallas_call(
         functools.partial(kernel, sizes),
         out_shape=jax.ShapeDtypeStruct((comps, layers, rows, cols), f32),
-        in_specs=[
-            anywhere,
-            pl.BlockSpec(memory_space=pltpu.SMEM),
-            anywhere,
-            anywhere,
-            anywhere,
-        ],
+        in_specs=[anywhere] * 5,
         out_specs=pl.BlockSpec(memory_space=pltpu.VMEM),
         scratch_shapes=[
             vmem((members, comps, layers + 2, deep, cols), f32),
@@ -683,6 +711,7 @@
             vmem(friction_table.shape, f32),
             vmem((rows, cols), jnp.int32),
             vmem((rows, cols), jnp.int32),
+            pltpu.SMEM((members,), jnp.int32),
             vmem((2 * comps, deep, cols), f32),
             vmem((2 * comps, deep, cols), f32),
             vmem((9, wide, cols), f32),
@@ -698,21 +727,24 @@
             vmem((4 * members, 8, cols), f32),
             vmem((2 * planeys, 1, cols), f32),
             vmem((planes, 1, cols), f32),
-            dma((4,)),
+            dma((5,)),
             dma((12,)),
             dma((12,)),
             pltpu.SemaphoreType.REGULAR((8,)),
             dma((3,)),
             dma((3,)),
-            dma((2 * planeys,)),
-            dma((2 * planeys,)),
-            dma((planes,)),
-            dma((planes,)),
+            dma((1,)),
+            dma((1,)),
+            dma((1,)),
+            dma((1,)),
         ],
         compiler_params=pltpu.CompilerParams(
             collective_id=0, has_side_effects=True, vmem_limit_bytes=48 * 1024 * 1024
         ),
-    )(u_prior, friction_rows, friction_table, bed_fixed, ice_mask)
+    )(*[
+        pltpu.with_memory_space_constraint(x, pltpu.HBM)
+        for x in (u_prior, friction_rows, friction_table, bed_fixed, ice_mask)
+    ])
 
 
 def solution(mesh):

time: 74 us -> 69.7 us (0.942)
  local copies, waits for them, and re-layouts: 4.59 us -> 0.67 us
    unnamed x11 -> x1, local copies, waits for them, and re-layouts: 4.59 us -> 0.67 us
where the time goes in v2:
time: 69.7 us; the launch traced here: 69.6 us
  Pallas kernels  68.9 us (99%)
    pallas_call x1, Pallas kernels, body(): pl.pallas_call(functools.partial(kernel, sizes), out_shape=jax.ShapeDtype...  68.9 us

profile of v2, /device:TPU:80, one launch (start us, length us, event | category | flops | bytes accessed | tf_op | source)
XLA Modules:
  0.0 69.6 jit_solution(2335403887959186849)
XLA Ops:
  0.0 68.9 %shard_map.55 = f32[2,10,16,128]{3,2,1,0:T(8,128)S(1)} custom-call(f32[2,2,10,16,128]{4,3,2,1,0:T(8,128)} %u_hbm.1, s32[2]{0:T(128)} %picks_hbm.1, f32[16,16,128]{2,1,0:T(8,128)} %table_hbm.1, s32[16,128]{1,0:T(8,128)} %bed_hbm.1, s32[16,128]{1,0:T(8,128)} %mask_hbm.1), custom_call_target="tpu_custom_call" | custom-call | tf_op jit(solution)/shard_map/pallas_call | solution.py:700
  68.9 0.7 copy.7

commit v3 on v2

--- a/solution.py
+++ b/solution.py
@@ -17,7 +17,7 @@
 along_z = 0.5
 along_x = (0.25, 0.125)
 along_y = (0.125, 0.25)
-BED, MASK, FRICTION = 4, 5, 6
+BED, MASK = 0, 1
 UNROLL = 10
 
 
@@ -50,6 +50,7 @@
     edge,
     fixed,
     roots,
+    step_y,
     tr,
     tp,
     tq,
@@ -96,20 +97,25 @@
                 flag = part if flag is None else jnp.logical_and(flag, part)
         return flag
 
+    def load_member(member):
+        return pltpu.make_async_copy(
+            u_hbm.at[member],
+            uw.at[member, :, pl.ds(1, layers), pl.ds(OWN, rows), :],
+            local_sem.at[member],
+        )
+
+    load_u = [load_member(member) for member in range(members)]
+    load_table = pltpu.make_async_copy(table_hbm, table, local_sem.at[members])
+    load_bed = pltpu.make_async_copy(bed_hbm, bed_in, local_sem.at[members + 1])
+    load_mask = pltpu.make_async_copy(mask_hbm, mask_in, local_sem.at[members + 2])
+    load_picks = pltpu.make_async_copy(picks_hbm, picks, local_sem.at[members + 3])
+    for load in (load_u[0], load_picks, load_table, load_bed, load_mask, *load_u[1:]):
+        load.start()
+
     barrier = pltpu.get_barrier_semaphore()
     for dx, dy in around:
         pl.semaphore_signal(barrier, inc=1, device_id=at(dx, dy), device_id_type=MESH)
     pl.semaphore_signal(barrier, inc=1, device_id=partner, device_id_type=MESH)
-
-    load_u = pltpu.make_async_copy(
-        u_hbm, uw.at[:, :, pl.ds(1, layers), pl.ds(OWN, rows), :], local_sem.at[0]
-    )
-    load_table = pltpu.make_async_copy(table_hbm, table, local_sem.at[1])
-    load_bed = pltpu.make_async_copy(bed_hbm, bed_in, local_sem.at[2])
-    load_mask = pltpu.make_async_copy(mask_hbm, mask_in, local_sem.at[3])
-    load_picks = pltpu.make_async_copy(picks_hbm, picks, local_sem.at[4])
-    for load in (load_u, load_bed, load_mask, load_picks, load_table):
-        load.start()
 
     for end_layer in (0, layers + 1):
         uw[:, :, end_layer, TOP:end, :] = jnp.zeros((members, comps, wide, cols), jnp.float32)
@@ -133,9 +139,10 @@
         def _():
             buffer[:, TOP:end, :] = jnp.zeros((buffer.shape[0], wide, cols), jnp.float32)
 
-    sends = []
-
-    def send(number, dx, dy, source, target):
+    sends = [[] for _ in range(members)]
+
+    def send(part, dx, dy, source, target):
+        number = sum(len(group) for group in sends)
         copy = pltpu.make_async_remote_copy(
             src_ref=source,
             dst_ref=target,
@@ -149,7 +156,10 @@
         def _():
             copy.start()
 
-        sends.append((copy, exists(dx, dy), exists(-dx, -dy)))
+        sends[part].append((copy, exists(dx, dy), exists(-dx, -dy)))
+
+    def first_field(member):
+        return 2 + member * (1 + comps)
 
     def row_range(dx):
         if dx < 0:
@@ -187,24 +197,8 @@
             if distance == reach:
                 greeted(number)
 
-    with scope("p0_load"):
-        load_u.wait()
-        load_bed.wait()
-        load_mask.wait()
-        load_picks.wait()
-        load_table.wait()
     lane = lax.broadcasted_iota(jnp.int32, (rows, cols), 1)
     group = lane // PITCH
-    bed_own = bed_in[...].astype(jnp.float32) * bed_unit
-    mask_own = mask_in[...].astype(jnp.float32)
-    mw[0, OWN : OWN + rows, :] = bed_own
-    mw[1, OWN : OWN + rows, :] = mask_own
-    for member in range(members):
-        chosen = table[picks[member]]
-        mw[2 + member, OWN : OWN + rows, :] = chosen
-        xo[FRICTION + member, OWN : OWN + rows, :] = jnp.where(
-            lane < PITCH, pltpu.roll(chosen, HALO, 1), 0.0
-        )
 
     def lane_packed(planes_of):
         packed = jnp.zeros((rows, cols), jnp.float32)
@@ -213,45 +207,72 @@
             packed = jnp.where(group == layer, turned, packed)
         return packed
 
-    xo[BED, OWN : OWN + rows, :] = lane_packed(lambda layer: bed_own)
-    xo[MASK, OWN : OWN + rows, :] = lane_packed(lambda layer: mask_own)
+    body = pl.ds(1, layers)
     for member in range(members):
+        with scope("p0_load"):
+            load_u[member].wait()
+        if member == 0:
+            with scope("p1_barrier"):
+                pl.semaphore_wait(barrier, len(around) + 1)
+        for dx in (-1, 1):
+            here, there = row_range(dx)
+            send(
+                member,
+                dx,
+                0,
+                uw.at[member, :, body, here, :],
+                uw.at[member, :, body, there, :],
+            )
+        base = first_field(member)
+        if member == 0:
+            greet_round(1)
+            load_bed.wait()
+            load_mask.wait()
+            load_picks.wait()
+            load_table.wait()
+            bed_own = bed_in[...].astype(jnp.float32) * bed_unit
+            mask_own = mask_in[...].astype(jnp.float32)
+            mw[0, OWN : OWN + rows, :] = bed_own
+            mw[1, OWN : OWN + rows, :] = mask_own
+            xo[BED, OWN : OWN + rows, :] = lane_packed(lambda layer: bed_own)
+            xo[MASK, OWN : OWN + rows, :] = lane_packed(lambda layer: mask_own)
+            for other in range(members):
+                chosen = table[picks[other]]
+                mw[2 + other, OWN : OWN + rows, :] = chosen
+                xo[first_field(other), OWN : OWN + rows, :] = jnp.where(
+                    lane < PITCH, pltpu.roll(chosen, HALO, 1), 0.0
+                )
         for comp in range(comps):
-            xo[member * comps + comp, OWN : OWN + rows, :] = lane_packed(
+            xo[base + 1 + comp, OWN : OWN + rows, :] = lane_packed(
                 lambda layer: uw[member, comp, 1 + layer, OWN : OWN + rows, :]
             )
-
-    with scope("p1_barrier"):
-        pl.semaphore_wait(barrier, len(around) + 1)
-    body = pl.ds(1, layers)
-    for dx in (-1, 1):
-        here, there = row_range(dx)
-        send(
-            0 if dx < 0 else 1,
-            dx,
-            0,
-            uw.at[:, :, body, here, :],
-            uw.at[:, :, body, there, :],
-        )
-    greet_round(1)
-    for number, (dx, dy) in enumerate(around):
-        here, there = row_range(dx)
-        target = xo if dy == 0 else (xr if dy < 0 else xl)
-        send(4 + number, dx, dy, xo.at[:, here, :], target.at[:, there, :])
-    for dx in (-1, 1):
-        here, there = row_range(dx)
-        send(2 if dx < 0 else 3, dx, 0, mw.at[:, here, :], mw.at[:, there, :])
+        low = 0 if member == 0 else base
+        part = pl.ds(low, base + 1 + comps - low)
+        for dx, dy in around:
+            here, there = row_range(dx)
+            target = xo if dy == 0 else (xr if dy < 0 else xl)
+            send(member, dx, dy, xo.at[part, here, :], target.at[part, there, :])
+        if member == 0:
+            for dx in (-1, 1):
+                here, there = row_range(dx)
+                send(0, dx, 0, mw.at[:, here, :], mw.at[:, there, :])
 
     with scope("p3_greeted1"):
         greeted_round(1)
     greet_round(2)
-
-    with scope("p4_halo"):
-        for copy, sent, arrives in sends:
-
-            @pl.when(arrives)
-            def _():
-                copy.wait_recv()
+    with scope("p5_greeted2"):
+        greeted_round(2)
+    greet_round(4)
+
+    def arrived(member):
+        with scope("p4_halo"):
+            for copy, sent, arrives in sends[member]:
+
+                @pl.when(arrives)
+                def _():
+                    copy.wait_recv()
+
+    arrived(0)
 
     lane = lax.broadcasted_iota(jnp.int32, (wide, cols), 1)
     first_lane = lane == 0
@@ -337,16 +358,16 @@
             total = total + value[low : low + 8]
         return total
 
-    def sample(member, carry):
-        base = member * comps
+    def sample(member):
+        base = first_field(member)
         for comp in range(comps):
-            pair = sides(base + comp)
+            pair = sides(base + 1 + comp)
             edge[EDGE_U + comp] = edges(pair)
             for side in range(2):
                 strip[comp * 2 + side, TOP:end, :] = pair[side]
         strip_roots = []
         strip_diag = []
-        friction_pair = sides(FRICTION + member)
+        friction_pair = sides(base)
         for side in range(2):
             value = [strip[comp * 2 + side, TOP:end, :] for comp in range(comps)]
             step_i = [
@@ -392,34 +413,42 @@
             ]
             edge[EDGE_2 + comp] = edges([strip_roots[side] * image[side] for side in range(2)])
 
-        def roots_and_start(layer, carry):
-            here = fixed[0]
-            value = [uw[member, comp, layer + 1, TOP:end, :] for comp in range(comps)]
+        for comp in range(comps):
+            for layer in range(layers):
+                plus, minus = y_pair(
+                    uw[member, comp, layer + 1, TOP:end, :],
+                    turned_edge(edge[EDGE_U + comp], layer),
+                )
+                step_y[comp, layer] = plus - minus
+        for layer in range(layers):
             step_i = [
                 uw[member, comp, layer + 1, TOP + 1 : end + 1, :]
                 - uw[member, comp, layer + 1, TOP - 1 : end - 1, :]
                 for comp in range(comps)
             ]
-            step_j = []
-            for comp in range(comps):
-                plus, minus = y_pair(value[comp], turned_edge(edge[EDGE_U + comp], layer))
-                step_j.append(plus - minus)
             step_z = [
                 uw[member, comp, layer + 2, TOP:end, :] - uw[member, comp, layer, TOP:end, :]
                 for comp in range(comps)
             ]
-            root = here * power(
-                strain4_of(step_i[0], step_i[1], step_j[0], step_j[1], step_z[0], step_z[1])
-            )
-            roots[layer] = root
+            roots[layer] = fixed[0] * power(
+                strain4_of(
+                    step_i[0],
+                    step_i[1],
+                    step_y[0, layer],
+                    step_y[1, layer],
+                    step_z[0],
+                    step_z[1],
+                )
+            )
+        for layer in range(layers):
+            root = roots[layer]
             plus, minus = y_pair(root, turned_edge(edge[EDGE_R], layer))
             both = plus + minus
             for comp in range(comps):
                 tr[comp, layer + 1, TOP:end, :] = root + along_y[comp] * both
-                field = root * (here * value[comp])
+                field = root * (fixed[0] * uw[member, comp, layer + 1, TOP:end, :])
                 plus, minus = y_pair(field, turned_edge(edge[EDGE_0 + comp], layer))
                 tp[comp, layer + 1, TOP:end, :] = field + along_y[comp] * (plus + minus)
-            return carry
 
         def x_sum(buffer, comp, layer):
             return buffer[comp, layer, TOP:end, :] + along_x[comp] * (
@@ -427,8 +456,6 @@
                 + buffer[comp, layer, TOP - 1 : end - 1, :]
             )
 
-        with scope("q1_roots"):
-            lax.fori_loop(0, layers, roots_and_start, 0, unroll=UNROLL)
         slot = members * ens + member
         empty = jnp.zeros((wide, cols), jnp.float32)
 
@@ -526,17 +553,34 @@
             )
         for number, value in enumerate((gram_rr, gram_ra, gram_aa, gram_ab)):
             gram[4 * member + number] = value
-        return carry
-
-    with scope("p5_greeted2"):
-        greeted_round(2)
-    greet_round(4)
-
-    def one_sample(member, carry):
-        sample(member, carry)
-
-        @pl.when(member == 0)
-        def _():
+
+    def to_partner(number, source, target):
+        copy = pltpu.make_async_remote_copy(
+            src_ref=source,
+            dst_ref=target,
+            send_sem=pair_send.at[number],
+            recv_sem=pair_recv.at[number],
+            device_id=partner,
+            device_id_type=MESH,
+        )
+        copy.start()
+        fields.append(copy)
+
+    fields = []
+    inner = pl.ds(HALO, rows)
+
+    def share_member(member):
+        slot = members * ens + member
+        for number, buffer in enumerate((all_residual, all_image)):
+            block = buffer.at[slot, :, :, inner, :]
+            to_partner(2 * member + number, block, block)
+
+    for member in range(members):
+        if member > 0:
+            arrived(member)
+        with scope("p6_sample"):
+            sample(member)
+        if member == 0:
             with scope("p6_greeted4"):
                 for reach in (4, 8, 16):
                     greeted_round(reach)
@@ -545,11 +589,8 @@
             pl.semaphore_signal(
                 hand_sem.at[len(hands)], inc=1, device_id=partner, device_id_type=MESH
             )
-
-        return carry
-
-    with scope("p6_samples"):
-        lax.fori_loop(0, members, one_sample, 0)
+        if member < members - 1:
+            share_member(member)
 
     lines = 4 * members
     total = jnp.sum(gram[...], axis=1)
@@ -593,9 +634,6 @@
         message,
     )
 
-    mine = pl.ds(members * ens, members)
-    inner = pl.ds(HALO, rows)
-    fields = []
     for comp in range(comps):
         for layer in range(layers):
             total = None
@@ -603,29 +641,12 @@
                 start = mw[1, OWN : OWN + rows, :] * uw[member, comp, layer + 1, OWN : OWN + rows, :]
                 total = start if total is None else total + start
             all_start[ens, comp, layer] = total
-    for number, (source, target) in enumerate(
-        (
-            (all_residual.at[mine, :, :, inner, :],) * 2,
-            (all_image.at[mine, :, :, inner, :],) * 2,
-            (all_start.at[ens],) * 2,
-        )
-    ):
-        copy = pltpu.make_async_remote_copy(
-            src_ref=source,
-            dst_ref=target,
-            send_sem=pair_send.at[number],
-            recv_sem=pair_recv.at[number],
-            device_id=partner,
-            device_id_type=MESH,
-        )
-        copy.start()
-        fields.append(copy)
-
-    for copy, sent, arrives in sends:
-
-        @pl.when(sent)
-        def _():
-            copy.wait_send()
+    for part in sends:
+        for copy, sent, arrives in part:
+
+            @pl.when(sent)
+            def _():
+                copy.wait_send()
 
     with scope("p8_ary"):
         copies_y.wait_recv()
@@ -638,9 +659,11 @@
         x_recv,
         jnp.sum(ring_y[...], axis=0),
     )
+    share_member(members - 1)
+    to_partner(2 * members, all_start.at[ens], all_start.at[ens])
+    copies_y.wait_send()
     for copy in fields:
         copy.wait_recv()
-    for copy in fields + [copies_y]:
         copy.wait_send()
     with scope("p9_arx"):
         copies_x.wait_recv()
@@ -694,7 +717,7 @@
     samples = 2 * members
     f32 = jnp.float32
     anywhere = pl.BlockSpec(memory_space=pltpu.HBM)
-    fields = FRICTION + members
+    fields = 2 + members * (1 + comps)
     vmem = pltpu.VMEM
     dma = pltpu.SemaphoreType.DMA
     return pl.pallas_call(
@@ -717,6 +740,7 @@
             vmem((9, wide, cols), f32),
             vmem((9, wide, cols), f32),
             vmem((layers, wide, cols), f32),
+            vmem((comps, layers, wide, cols), f32),
             vmem((comps, layers + 2, deep, cols), f32),
             vmem((comps, layers + 2, deep, cols), f32),
             vmem((comps, layers + 2, deep, cols), f32),
@@ -727,12 +751,12 @@
             vmem((4 * members, 8, cols), f32),
             vmem((2 * planeys, 1, cols), f32),
             vmem((planes, 1, cols), f32),
-            dma((5,)),
-            dma((12,)),
-            dma((12,)),
+            dma((members + 4,)),
+            dma((2 + 10 * members,)),
+            dma((2 + 10 * members,)),
             pltpu.SemaphoreType.REGULAR((8,)),
-            dma((3,)),
-            dma((3,)),
+            dma((2 * members + 1,)),
+            dma((2 * members + 1,)),
             dma((1,)),
             dma((1,)),
             dma((1,)),

time: 69.7 us -> 67.6 us (0.970)
  Pallas kernels: 68.9 us -> 66.7 us
    pallas_call x1, Pallas kernels: 68.9 us -> 66.7 us  [body(): pl.pallas_call(functools.partial(kernel, sizes), out_shape=jax.ShapeDtype...]
where the time goes in v3:
time: 67.6 us; the launch traced here: 67.4 us
  Pallas kernels  66.7 us (99%)
    pallas_call x1, Pallas kernels, body(): pl.pallas_call(functools.partial(kernel, sizes), out_shape=jax.ShapeDtype...  66.7 us

profile of v3, /device:TPU:80, one launch (start us, length us, event | category | flops | bytes accessed | tf_op | source)
XLA Modules:
  0.0 67.4 jit_solution(10639674625225424919)
XLA Ops:
  0.0 66.7 %shard_map.55 = f32[2,10,16,128]{3,2,1,0:T(8,128)S(1)} custom-call(f32[2,2,10,16,128]{4,3,2,1,0:T(8,128)} %u_hbm.1, s32[2]{0:T(128)} %picks_hbm.1, f32[16,16,128]{2,1,0:T(8,128)} %table_hbm.1, s32[16,128]{1,0:T(8,128)} %bed_hbm.1, s32[16,128]{1,0:T(8,128)} %mask_hbm.1), custom_call_target="tpu_custom_call" | custom-call | tf_op jit(solution)/shard_map/pallas_call | solution.py:723
  66.8 0.7 copy.7

commit v4 on v3

--- a/solution.py
+++ b/solution.py
@@ -17,7 +17,7 @@
 along_z = 0.5
 along_x = (0.25, 0.125)
 along_y = (0.125, 0.25)
-BED, MASK = 0, 1
+MASK = 0
 UNROLL = 10
 
 
@@ -47,6 +47,8 @@
     picks,
     strip,
     shifted,
+    strip_kept,
+    tally,
     edge,
     fixed,
     roots,
@@ -97,6 +99,14 @@
                 flag = part if flag is None else jnp.logical_and(flag, part)
         return flag
 
+    bed_field = 1 + comps
+
+    def friction_field(member):
+        return bed_field + 1 + member * (1 + comps) - (comps if member > 0 else 0)
+
+    def u_field(member):
+        return 1 if member == 0 else friction_field(member) + 1
+
     def load_member(member):
         return pltpu.make_async_copy(
             u_hbm.at[member],
@@ -105,11 +115,13 @@
         )
 
     load_u = [load_member(member) for member in range(members)]
-    load_table = pltpu.make_async_copy(table_hbm, table, local_sem.at[members])
-    load_bed = pltpu.make_async_copy(bed_hbm, bed_in, local_sem.at[members + 1])
-    load_mask = pltpu.make_async_copy(mask_hbm, mask_in, local_sem.at[members + 2])
-    load_picks = pltpu.make_async_copy(picks_hbm, picks, local_sem.at[members + 3])
-    for load in (load_u[0], load_picks, load_table, load_bed, load_mask, *load_u[1:]):
+    load_picks = pltpu.make_async_copy(picks_hbm, picks, local_sem.at[members])
+    load_maps = [
+        pltpu.make_async_copy(source, target, local_sem.at[members + 1])
+        for source, target in ((table_hbm, table), (bed_hbm, bed_in), (mask_hbm, mask_in))
+    ]
+    maps_rows = (table.shape[0] + 2) * rows
+    for load in (load_u[0], load_picks, *load_maps, *load_u[1:]):
         load.start()
 
     barrier = pltpu.get_barrier_semaphore()
@@ -139,27 +151,60 @@
         def _():
             buffer[:, TOP:end, :] = jnp.zeros((buffer.shape[0], wide, cols), jnp.float32)
 
-    sends = [[] for _ in range(members)]
-
-    def send(part, dx, dy, source, target):
-        number = sum(len(group) for group in sends)
-        copy = pltpu.make_async_remote_copy(
-            src_ref=source,
-            dst_ref=target,
-            send_sem=halo_send.at[number],
-            recv_sem=halo_recv.at[number],
-            device_id=at(dx, dy),
-            device_id_type=MESH,
-        )
+    def kind(dx, dy):
+        return "both" if dx != 0 and dy != 0 else ("x" if dx != 0 else "y")
+
+    def send(part, dx, dy, *pairs):
+        copies = [
+            pltpu.make_async_remote_copy(
+                src_ref=source,
+                dst_ref=target,
+                send_sem=halo_send.at[0],
+                recv_sem=halo_recv.at[part],
+                device_id=at(dx, dy),
+                device_id_type=MESH,
+            )
+            for source, target in pairs
+        ]
 
         @pl.when(exists(dx, dy))
         def _():
-            copy.start()
-
-        sends[part].append((copy, exists(dx, dy), exists(-dx, -dy)))
-
-    def first_field(member):
-        return 2 + member * (1 + comps)
+            for copy in copies:
+                copy.start()
+
+        if dx >= 0 and dy >= 0:
+            for source, _ in pairs:
+                count = 1
+                for size in source.shape[:-1]:
+                    count *= size
+                rows_of[part][kind(dx, dy)] += count
+
+    rows_of = [{"x": 0, "y": 0, "both": 0} for _ in range(1 + members)]
+
+    def each_total(counts, action):
+        ends_x = jnp.logical_or(plane == 0, plane == planes - 1)
+        ends_y = jnp.logical_or(planey == 0, planey == planeys - 1)
+        for many_x in (1, 2):
+            for many_y in (1, 2):
+                total = many_x * counts["x"] + many_y * counts["y"]
+                total += many_x * many_y * counts["both"]
+                here_x = ends_x if many_x == 1 else jnp.logical_not(ends_x)
+                here_y = ends_y if many_y == 1 else jnp.logical_not(ends_y)
+
+                @pl.when(jnp.logical_and(here_x, here_y))
+                def _():
+                    action(total)
+
+    def counted(total, part):
+        block = tally.at[pl.ds(0, total)]
+        return pltpu.make_async_remote_copy(
+            src_ref=block,
+            dst_ref=block,
+            send_sem=halo_send.at[0],
+            recv_sem=halo_recv.at[part],
+            device_id=partner,
+            device_id_type=MESH,
+        )
 
     def row_range(dx):
         if dx < 0:
@@ -208,54 +253,63 @@
         return packed
 
     body = pl.ds(1, layers)
-    for member in range(members):
-        with scope("p0_load"):
-            load_u[member].wait()
-        if member == 0:
-            with scope("p1_barrier"):
-                pl.semaphore_wait(barrier, len(around) + 1)
+
+    def send_u(part, member):
         for dx in (-1, 1):
             here, there = row_range(dx)
             send(
-                member,
+                part,
                 dx,
                 0,
-                uw.at[member, :, body, here, :],
-                uw.at[member, :, body, there, :],
-            )
-        base = first_field(member)
-        if member == 0:
-            greet_round(1)
-            load_bed.wait()
-            load_mask.wait()
-            load_picks.wait()
-            load_table.wait()
-            bed_own = bed_in[...].astype(jnp.float32) * bed_unit
-            mask_own = mask_in[...].astype(jnp.float32)
-            mw[0, OWN : OWN + rows, :] = bed_own
-            mw[1, OWN : OWN + rows, :] = mask_own
-            xo[BED, OWN : OWN + rows, :] = lane_packed(lambda layer: bed_own)
-            xo[MASK, OWN : OWN + rows, :] = lane_packed(lambda layer: mask_own)
-            for other in range(members):
-                chosen = table[picks[other]]
-                mw[2 + other, OWN : OWN + rows, :] = chosen
-                xo[first_field(other), OWN : OWN + rows, :] = jnp.where(
-                    lane < PITCH, pltpu.roll(chosen, HALO, 1), 0.0
-                )
+                (uw.at[member, :, body, here, :], uw.at[member, :, body, there, :]),
+            )
+
+    def pack_u(member):
         for comp in range(comps):
-            xo[base + 1 + comp, OWN : OWN + rows, :] = lane_packed(
+            xo[u_field(member) + comp, OWN : OWN + rows, :] = lane_packed(
                 lambda layer: uw[member, comp, 1 + layer, OWN : OWN + rows, :]
             )
-        low = 0 if member == 0 else base
-        part = pl.ds(low, base + 1 + comps - low)
-        for dx, dy in around:
+
+    def send_packed(part, low, count, map_low, map_count):
+        fields_here = pl.ds(low, count)
+        maps_here = pl.ds(map_low, map_count)
+        for dx, dy in sorted(around, key=lambda d: -abs(d[0])):
             here, there = row_range(dx)
             target = xo if dy == 0 else (xr if dy < 0 else xl)
-            send(member, dx, dy, xo.at[part, here, :], target.at[part, there, :])
-        if member == 0:
-            for dx in (-1, 1):
-                here, there = row_range(dx)
-                send(0, dx, 0, mw.at[:, here, :], mw.at[:, there, :])
+            pairs = [(xo.at[fields_here, here, :], target.at[fields_here, there, :])]
+            if dy == 0:
+                pairs.append((mw.at[maps_here, here, :], mw.at[maps_here, there, :]))
+            send(part, dx, dy, *pairs)
+
+    with scope("p0_load"):
+        load_u[0].wait()
+    with scope("p1_barrier"):
+        pl.semaphore_wait(barrier, len(around) + 1)
+    send_u(0, 0)
+    block = tally.at[pl.ds(0, maps_rows)]
+    pltpu.make_async_copy(block, block, local_sem.at[members + 1]).wait()
+    load_picks.wait()
+    mask_own = mask_in[...].astype(jnp.float32)
+    bed_own = bed_in[...].astype(jnp.float32) * bed_unit
+    mw[0, OWN : OWN + rows, :] = mask_own
+    xo[MASK, OWN : OWN + rows, :] = lane_packed(lambda layer: mask_own)
+    pack_u(0)
+    send_packed(0, 0, 1 + comps, 0, 1)
+    greet_round(1)
+    mw[1, OWN : OWN + rows, :] = bed_own
+    xo[bed_field, OWN : OWN + rows, :] = lane_packed(lambda layer: bed_own)
+    for member in range(members):
+        chosen = table[picks[member]]
+        mw[2 + member, OWN : OWN + rows, :] = chosen
+        xo[friction_field(member), OWN : OWN + rows, :] = jnp.where(
+            lane < PITCH, pltpu.roll(chosen, HALO, 1), 0.0
+        )
+    send_packed(1, bed_field, 2, 1, 2)
+    for member in range(1, members):
+        load_u[member].wait()
+        send_u(1 + member, member)
+        pack_u(member)
+        send_packed(1 + member, friction_field(member), 1 + comps, 2 + member, 1)
 
     with scope("p3_greeted1"):
         greeted_round(1)
@@ -263,14 +317,13 @@
     with scope("p5_greeted2"):
         greeted_round(2)
     greet_round(4)
-
-    def arrived(member):
-        with scope("p4_halo"):
-            for copy, sent, arrives in sends[member]:
-
-                @pl.when(arrives)
-                def _():
-                    copy.wait_recv()
+    pl.semaphore_signal(
+        hand_sem.at[len(hands)], inc=1, device_id=partner, device_id_type=MESH
+    )
+
+    def arrived(part):
+        with scope("p4_halo%d" % part):
+            each_total(rows_of[part], lambda total: counted(total, part).wait_recv())
 
     arrived(0)
 
@@ -307,21 +360,26 @@
     def turned_edge(value, layer):
         return pltpu.roll(value, cols - HALO - PITCH * layer, 1)
 
-    mask_main = mw[1, TOP:end, :]
-    bed_plus, bed_minus = y_pair(mw[0, TOP:end, :], turned_edge(edges(sides(BED)), 0))
-    scale = -(mask_main * thickness)
+    mask_main = mw[0, TOP:end, :]
     fixed[0] = mask_main
-    fixed[1] = scale * ((mw[0, TOP + 1 : end + 1, :] - mw[0, TOP - 1 : end - 1, :]) * 0.5)
-    fixed[2] = scale * ((bed_plus - bed_minus) * 0.5)
-    strip_force = []
-    for side, (bed_here, mask_here) in enumerate(zip(sides(BED), sides(MASK))):
-        shifted[side, TOP:end, :] = bed_here
-        down = shifted[side, TOP + 1 : end + 1, :] - shifted[side, TOP - 1 : end - 1, :]
-        flat = pltpu.roll(bed_here, cols - 1, 1) - pltpu.roll(bed_here, 1, 1)
-        scale = -(mask_here * thickness)
+    for side, mask_here in enumerate(sides(MASK)):
         fixed[3 + side] = mask_here
-        fixed[5 + side] = scale * (down * 0.5)
-        fixed[7 + side] = scale * (flat * 0.5)
+
+    def forces():
+        bed_pair = sides(bed_field)
+        bed_plus, bed_minus = y_pair(mw[1, TOP:end, :], turned_edge(edges(bed_pair), 0))
+        scale = -(fixed[0] * thickness)
+        fixed[1] = scale * (
+            (mw[1, TOP + 1 : end + 1, :] - mw[1, TOP - 1 : end - 1, :]) * 0.5
+        )
+        fixed[2] = scale * ((bed_plus - bed_minus) * 0.5)
+        for side, bed_here in enumerate(bed_pair):
+            shifted[side, TOP:end, :] = bed_here
+            down = shifted[side, TOP + 1 : end + 1, :] - shifted[side, TOP - 1 : end - 1, :]
+            flat = pltpu.roll(bed_here, cols - 1, 1) - pltpu.roll(bed_here, 1, 1)
+            scale = -(fixed[3 + side] * thickness)
+            fixed[5 + side] = scale * (down * 0.5)
+            fixed[7 + side] = scale * (flat * 0.5)
 
     def power(strain4):
         return jnp.exp(jnp.log(strain4 * 0.25 + 0.1) * (-1.0 / 6.0))
@@ -358,16 +416,13 @@
             total = total + value[low : low + 8]
         return total
 
-    def sample(member):
-        base = first_field(member)
+    def strip_start(member):
         for comp in range(comps):
-            pair = sides(base + 1 + comp)
+            pair = sides(u_field(member) + comp)
             edge[EDGE_U + comp] = edges(pair)
             for side in range(2):
                 strip[comp * 2 + side, TOP:end, :] = pair[side]
         strip_roots = []
-        strip_diag = []
-        friction_pair = sides(base)
         for side in range(2):
             value = [strip[comp * 2 + side, TOP:end, :] for comp in range(comps)]
             step_i = [
@@ -377,32 +432,47 @@
             ]
             step_j = [pltpu.roll(v, cols - 1, 1) - pltpu.roll(v, 1, 1) for v in value]
             step_z = [pltpu.roll(v, cols - PITCH, 1) - pltpu.roll(v, PITCH, 1) for v in value]
-            here = fixed[3 + side]
             strip_roots.append(
-                here
+                fixed[3 + side]
                 * power(
                     strain4_of(
                         step_i[0], step_i[1], step_j[0], step_j[1], step_z[0], step_z[1]
                     )
                 )
             )
-            strip_diag.append(here * friction_pair[side] + (1.0 - here))
+            strip_kept[side] = strip_roots[side]
         edge[EDGE_R] = edges(strip_roots)
         for comp in range(comps):
             around_roots = strip_k(strip_roots, comp, comp * 2)
-            start = [
-                fixed[3 + side] * strip[comp * 2 + side, TOP:end, :] for side in range(2)
+            field = [
+                strip_roots[side] * (fixed[3 + side] * strip[comp * 2 + side, TOP:end, :])
+                for side in range(2)
             ]
-            field = [strip_roots[side] * start[side] for side in range(2)]
             edge[EDGE_0 + comp] = edges(field)
-            near = strip_k(field, comp, comp * 2)
-            four = [4.0 * strip_roots[side] for side in range(2)]
+            near = strip_k(field, comp, 4 + comp * 2)
+            for side in range(2):
+                strip_kept[2 + 4 * comp + side] = around_roots[side]
+                strip_kept[4 + 4 * comp + side] = near[side]
+
+    def strip_end(member):
+        strip_roots = [strip_kept[side] for side in range(2)]
+        four = [4.0 * root for root in strip_roots]
+        friction_pair = sides(friction_field(member))
+        diag = [
+            fixed[3 + side] * friction_pair[side] + (1.0 - fixed[3 + side])
+            for side in range(2)
+        ]
+        for comp in range(comps):
             main = [
-                four[side] * around_roots[side] + strip_diag[side] for side in range(2)
+                four[side] * strip_kept[2 + 4 * comp + side] + diag[side]
+                for side in range(2)
             ]
             residual = [
                 fixed[5 + 2 * comp + side]
-                - (main[side] * start[side] - four[side] * near[side])
+                - (
+                    main[side] * (fixed[3 + side] * strip[comp * 2 + side, TOP:end, :])
+                    - four[side] * strip_kept[4 + 4 * comp + side]
+                )
                 for side in range(2)
             ]
             field = [strip_roots[side] * residual[side] for side in range(2)]
@@ -413,6 +483,7 @@
             ]
             edge[EDGE_2 + comp] = edges([strip_roots[side] * image[side] for side in range(2)])
 
+    def share_start(member):
         for comp in range(comps):
             for layer in range(layers):
                 plus, minus = y_pair(
@@ -450,12 +521,13 @@
                 plus, minus = y_pair(field, turned_edge(edge[EDGE_0 + comp], layer))
                 tp[comp, layer + 1, TOP:end, :] = field + along_y[comp] * (plus + minus)
 
-        def x_sum(buffer, comp, layer):
-            return buffer[comp, layer, TOP:end, :] + along_x[comp] * (
-                buffer[comp, layer, TOP + 1 : end + 1, :]
-                + buffer[comp, layer, TOP - 1 : end - 1, :]
-            )
-
+    def x_sum(buffer, comp, layer):
+        return buffer[comp, layer, TOP:end, :] + along_x[comp] * (
+            buffer[comp, layer, TOP + 1 : end + 1, :]
+            + buffer[comp, layer, TOP - 1 : end - 1, :]
+        )
+
+    def share_end(member):
         slot = members * ens + member
         empty = jnp.zeros((wide, cols), jnp.float32)
 
@@ -554,41 +626,35 @@
         for number, value in enumerate((gram_rr, gram_ra, gram_aa, gram_ab)):
             gram[4 * member + number] = value
 
-    def to_partner(number, source, target):
-        copy = pltpu.make_async_remote_copy(
-            src_ref=source,
-            dst_ref=target,
-            send_sem=pair_send.at[number],
-            recv_sem=pair_recv.at[number],
+    def to_partner(block):
+        pltpu.make_async_remote_copy(
+            src_ref=block,
+            dst_ref=block,
+            send_sem=pair_send.at[0],
+            recv_sem=pair_recv.at[0],
             device_id=partner,
             device_id_type=MESH,
-        )
-        copy.start()
-        fields.append(copy)
-
-    fields = []
+        ).start()
+
     inner = pl.ds(HALO, rows)
 
     def share_member(member):
         slot = members * ens + member
-        for number, buffer in enumerate((all_residual, all_image)):
-            block = buffer.at[slot, :, :, inner, :]
-            to_partner(2 * member + number, block, block)
+        for buffer in (all_residual, all_image):
+            to_partner(buffer.at[slot, :, :, inner, :])
 
     for member in range(members):
         if member > 0:
-            arrived(member)
-        with scope("p6_sample"):
-            sample(member)
+            arrived(1 + member)
+        with scope("q0_start"):
+            strip_start(member)
+            share_start(member)
         if member == 0:
-            with scope("p6_greeted4"):
-                for reach in (4, 8, 16):
-                    greeted_round(reach)
-                    if reach > 2:
-                        greet_round(2 * reach)
-            pl.semaphore_signal(
-                hand_sem.at[len(hands)], inc=1, device_id=partner, device_id_type=MESH
-            )
+            arrived(1)
+            forces()
+        with scope("q1_end"):
+            strip_end(member)
+            share_end(member)
         if member < members - 1:
             share_member(member)
 
@@ -638,18 +704,20 @@
         for layer in range(layers):
             total = None
             for member in range(members):
-                start = mw[1, OWN : OWN + rows, :] * uw[member, comp, layer + 1, OWN : OWN + rows, :]
+                start = mw[0, OWN : OWN + rows, :] * uw[member, comp, layer + 1, OWN : OWN + rows, :]
                 total = start if total is None else total + start
             all_start[ens, comp, layer] = total
-    for part in sends:
-        for copy, sent, arrives in part:
-
-            @pl.when(sent)
-            def _():
-                copy.wait_send()
-
+    everything = {
+        name: sum(counts[name] for counts in rows_of) for name in ("x", "y", "both")
+    }
+    each_total(everything, lambda total: counted(total, 0).wait_send())
     with scope("p8_ary"):
         copies_y.wait_recv()
+    with scope("p6_greeted4"):
+        for reach in (4, 8, 16):
+            greeted_round(reach)
+            if reach > 2:
+                greet_round(2 * reach)
     copies_x = exchange(
         ring_x,
         plane,
@@ -660,11 +728,19 @@
         jnp.sum(ring_y[...], axis=0),
     )
     share_member(members - 1)
-    to_partner(2 * members, all_start.at[ens], all_start.at[ens])
+    to_partner(all_start.at[ens])
     copies_y.wait_send()
-    for copy in fields:
-        copy.wait_recv()
-        copy.wait_send()
+    block = all_residual.at[:, :, :, pl.ds(0, (2 * members + 1) * rows // (2 * members)), :]
+    fields = pltpu.make_async_remote_copy(
+        src_ref=block,
+        dst_ref=block,
+        send_sem=pair_send.at[0],
+        recv_sem=pair_recv.at[0],
+        device_id=partner,
+        device_id_type=MESH,
+    )
+    fields.wait_send()
+    fields.wait_recv()
     with scope("p9_arx"):
         copies_x.wait_recv()
     sums = jnp.sum(ring_x[...], axis=0)
@@ -736,7 +812,9 @@
             vmem((rows, cols), jnp.int32),
             pltpu.SMEM((members,), jnp.int32),
             vmem((2 * comps, deep, cols), f32),
-            vmem((2 * comps, deep, cols), f32),
+            vmem((4 * comps, deep, cols), f32),
+            vmem((2 + 4 * comps, wide, cols), f32),
+            vmem((1536, cols), f32),
             vmem((9, wide, cols), f32),
             vmem((9, wide, cols), f32),
             vmem((layers, wide, cols), f32),
@@ -751,12 +829,12 @@
             vmem((4 * members, 8, cols), f32),
             vmem((2 * planeys, 1, cols), f32),
             vmem((planes, 1, cols), f32),
-            dma((members + 4,)),
-            dma((2 + 10 * members,)),
-            dma((2 + 10 * members,)),
-            pltpu.SemaphoreType.REGULAR((8,)),
-            dma((2 * members + 1,)),
-            dma((2 * members + 1,)),
+            dma((members + 2,)),
+            dma((1,)),
+            dma((1 + members,)),
+            pltpu.SemaphoreType.REGULAR((6,)),
+            dma((1,)),
+            dma((1,)),
             dma((1,)),
             dma((1,)),
             dma((1,)),

time: 67.6 us -> 64.6 us (0.956)
  Pallas kernels: 66.7 us -> 63.8 us
    pallas_call x1, Pallas kernels: 66.7 us -> 63.8 us  [body(): pl.pallas_call(functools.partial(kernel, sizes), out_shape=jax.ShapeDtype...]
where the time goes in v4:
time: 64.6 us; the launch traced here: 64.4 us
  Pallas kernels  63.8 us (99%)
  local copies, waits for them, and re-layouts  0.67 us (1%)
    pallas_call x1, Pallas kernels, body(): pl.pallas_call(functools.partial(kernel, sizes), out_shape=jax.ShapeDtype...  63.8 us

profile of v4, /device:TPU:80, one launch (start us, length us, event | category | flops | bytes accessed | tf_op | source)
XLA Modules:
  0.0 64.4 jit_solution(2750134544818577387)
XLA Ops:
  0.0 63.8 %shard_map.55 = f32[2,10,16,128]{3,2,1,0:T(8,128)S(1)} custom-call(f32[2,2,10,16,128]{4,3,2,1,0:T(8,128)} %u_hbm.1, s32[2]{0:T(128)} %picks_hbm.1, f32[16,16,128]{2,1,0:T(8,128)} %table_hbm.1, s32[16,128]{1,0:T(8,128)} %bed_hbm.1, s32[16,128]{1,0:T(8,128)} %mask_hbm.1), custom_call_target="tpu_custom_call" | custom-call | tf_op jit(solution)/shard_map/pallas_call | solution.py:799
  63.8 0.7 %copy.7 = f32[2,10,16,128]{3,2,1,0:T(8,128)} copy(f32[2,10,16,128]{3,2,1,0:T(8,128)S(1)} %shard_map.55) | data formatting | bytes 327680

commit v5 on v4

--- a/solution.py
+++ b/solution.py
@@ -48,6 +48,7 @@
     strip,
     shifted,
     strip_kept,
+    lane_matrix,
     tally,
     edge,
     fixed,
@@ -325,6 +326,32 @@
         with scope("p4_halo%d" % part):
             each_total(rows_of[part], lambda total: counted(total, part).wait_recv())
 
+    bf16 = jnp.bfloat16
+    apart = lax.broadcasted_iota(jnp.int32, (cols, cols), 0) - lax.broadcasted_iota(
+        jnp.int32, (cols, cols), 1
+    )
+
+    def at_steps(step):
+        return jnp.where(apart == step, 1.0, 0.0)
+
+    near_z = at_steps(PITCH) + at_steps(-PITCH)
+    corners = (
+        at_steps(PITCH + 1) + at_steps(PITCH - 1) + at_steps(1 - PITCH) + at_steps(-PITCH - 1)
+    )
+    near_y = at_steps(1) + at_steps(-1)
+    lane_sums = [
+        at_steps(0)
+        + along_y[comp] * near_y
+        + along_z * near_z
+        + along_y[comp] * along_z * corners
+        for comp in range(comps)
+    ]
+    lane_steps = [at_steps(1) - at_steps(-1), at_steps(PITCH) - at_steps(-PITCH)]
+    for number, matrix in enumerate(lane_sums + lane_steps):
+        matrix = matrix.astype(bf16)
+        lane_matrix[number, :cols, :] = matrix
+        lane_matrix[number, cols:, :] = matrix
+
     arrived(0)
 
     lane = lax.broadcasted_iota(jnp.int32, (wide, cols), 1)
@@ -388,15 +415,21 @@
         shear = uj + vi
         return ui * ui + vj * vj + ui * vj + 0.25 * (shear * shear + (uz * uz + vz * vz))
 
+    def lane_halves(values):
+        stacked = jnp.concatenate(values, axis=0)
+        high = stacked.astype(bf16)
+        low = (stacked - high.astype(jnp.float32)).astype(bf16)
+        return jnp.concatenate([high, low], axis=1)
+
+    def lane_product(halves, number):
+        product = jnp.dot(
+            halves, lane_matrix[number], preferred_element_type=jnp.float32
+        )
+        return [product[low : low + wide] for low in range(0, product.shape[0], wide)]
+
     def strip_k(pair, comp, slot):
         result = []
-        for side, value in enumerate(pair):
-            value = value + along_y[comp] * (
-                pltpu.roll(value, cols - 1, 1) + pltpu.roll(value, 1, 1)
-            )
-            value = value + along_z * (
-                pltpu.roll(value, cols - PITCH, 1) + pltpu.roll(value, PITCH, 1)
-            )
+        for side, value in enumerate(lane_product(lane_halves(pair), comp)):
             shifted[slot + side, TOP:end, :] = value
             result.append(
                 value
@@ -423,15 +456,17 @@
             for side in range(2):
                 strip[comp * 2 + side, TOP:end, :] = pair[side]
         strip_roots = []
+        halves = lane_halves([strip[k, TOP:end, :] for k in range(2 * comps)])
+        steps_j = lane_product(halves, comps)
+        steps_z = lane_product(halves, comps + 1)
         for side in range(2):
-            value = [strip[comp * 2 + side, TOP:end, :] for comp in range(comps)]
             step_i = [
                 strip[comp * 2 + side, TOP + 1 : end + 1, :]
                 - strip[comp * 2 + side, TOP - 1 : end - 1, :]
                 for comp in range(comps)
             ]
-            step_j = [pltpu.roll(v, cols - 1, 1) - pltpu.roll(v, 1, 1) for v in value]
-            step_z = [pltpu.roll(v, cols - PITCH, 1) - pltpu.roll(v, PITCH, 1) for v in value]
+            step_j = [steps_j[comp * 2 + side] for comp in range(comps)]
+            step_z = [steps_z[comp * 2 + side] for comp in range(comps)]
             strip_roots.append(
                 fixed[3 + side]
                 * power(
@@ -669,9 +704,9 @@
     with scope("p7_hand"):
         pl.semaphore_wait(hand_sem.at[len(hands)], 1)
 
-    def exchange(ring, me, count, target, send_sem, recv_sem, value):
+    def exchange(ring, me, count, target, send_sem, recv_sem, value, sign=-1):
         ring[me] = value
-        for offset in sorted(range(1, count), key=lambda k: -min(k, count - k)):
+        for offset in sorted(range(1, count), key=lambda k: sign * min(k, count - k)):
             pltpu.make_async_remote_copy(
                 src_ref=ring.at[me],
                 dst_ref=ring.at[me],
@@ -700,6 +735,7 @@
         message,
     )
 
+    share_member(members - 1)
     for comp in range(comps):
         for layer in range(layers):
             total = None
@@ -707,6 +743,7 @@
                 start = mw[0, OWN : OWN + rows, :] * uw[member, comp, layer + 1, OWN : OWN + rows, :]
                 total = start if total is None else total + start
             all_start[ens, comp, layer] = total
+    to_partner(all_start.at[ens])
     everything = {
         name: sum(counts[name] for counts in rows_of) for name in ("x", "y", "both")
     }
@@ -726,9 +763,8 @@
         x_send,
         x_recv,
         jnp.sum(ring_y[...], axis=0),
+        sign=1,
     )
-    share_member(members - 1)
-    to_partner(all_start.at[ens])
     copies_y.wait_send()
     block = all_residual.at[:, :, :, pl.ds(0, (2 * members + 1) * rows // (2 * members)), :]
     fields = pltpu.make_async_remote_copy(
@@ -814,6 +850,7 @@
             vmem((2 * comps, deep, cols), f32),
             vmem((4 * comps, deep, cols), f32),
             vmem((2 + 4 * comps, wide, cols), f32),
+            vmem((4, 2 * cols, cols), jnp.bfloat16),
             vmem((1536, cols), f32),
             vmem((9, wide, cols), f32),
             vmem((9, wide, cols), f32),

time: 64.6 us -> 63.6 us (0.985)
  Pallas kernels: 63.8 us -> 62.8 us
    pallas_call x1, Pallas kernels: 63.8 us -> 62.8 us  [body(): pl.pallas_call(functools.partial(kernel, sizes), out_shape=jax.ShapeDtype...]
where the time goes in v5:
time: 63.6 us; the launch traced here: 63.5 us
  Pallas kernels  62.8 us (99%)
  local copies, waits for them, and re-layouts  0.67 us (1%)
    pallas_call x1, Pallas kernels, body(): pl.pallas_call(functools.partial(kernel, sizes), out_shape=jax.ShapeDtype...  62.8 us

profile of v5, /device:TPU:80, one launch (start us, length us, event | category | flops | bytes accessed | tf_op | source)
XLA Modules:
  0.0 63.5 jit_solution(6001427590477070722)
XLA Ops:
  0.0 62.8 %shard_map.55 = f32[2,10,16,128]{3,2,1,0:T(8,128)S(1)} custom-call(f32[2,2,10,16,128]{4,3,2,1,0:T(8,128)} %u_hbm.1, s32[2]{0:T(128)} %picks_hbm.1, f32[16,16,128]{2,1,0:T(8,128)} %table_hbm.1, s32[16,128]{1,0:T(8,128)} %bed_hbm.1, s32[16,128]{1,0:T(8,128)} %mask_hbm.1), custom_call_target="tpu_custom_call" | custom-call | tf_op jit(solution)/shard_map/pallas_call | solution.py:835
  62.8 0.7 %copy.7 = f32[2,10,16,128]{3,2,1,0:T(8,128)} copy(f32[2,10,16,128]{3,2,1,0:T(8,128)S(1)} %shard_map.55) | data formatting | bytes 327680

commit v6 on v5

--- a/solution.py
+++ b/solution.py
@@ -180,7 +180,7 @@
                     count *= size
                 rows_of[part][kind(dx, dy)] += count
 
-    rows_of = [{"x": 0, "y": 0, "both": 0} for _ in range(1 + members)]
+    rows_of = [{"x": 0, "y": 0, "both": 0} for _ in range(2 + members)]
 
     def each_total(counts, action):
         ends_x = jnp.logical_or(plane == 0, plane == planes - 1)
@@ -286,7 +286,6 @@
         load_u[0].wait()
     with scope("p1_barrier"):
         pl.semaphore_wait(barrier, len(around) + 1)
-    send_u(0, 0)
     block = tally.at[pl.ds(0, maps_rows)]
     pltpu.make_async_copy(block, block, local_sem.at[members + 1]).wait()
     load_picks.wait()
@@ -296,6 +295,7 @@
     xo[MASK, OWN : OWN + rows, :] = lane_packed(lambda layer: mask_own)
     pack_u(0)
     send_packed(0, 0, 1 + comps, 0, 1)
+    send_u(1 + members, 0)
     greet_round(1)
     mw[1, OWN : OWN + rows, :] = bed_own
     xo[bed_field, OWN : OWN + rows, :] = lane_packed(lambda layer: bed_own)
@@ -315,12 +315,6 @@
     with scope("p3_greeted1"):
         greeted_round(1)
     greet_round(2)
-    with scope("p5_greeted2"):
-        greeted_round(2)
-    greet_round(4)
-    pl.semaphore_signal(
-        hand_sem.at[len(hands)], inc=1, device_id=partner, device_id_type=MESH
-    )
 
     def arrived(part):
         with scope("p4_halo%d" % part):
@@ -562,6 +556,13 @@
             + buffer[comp, layer, TOP - 1 : end - 1, :]
         )
 
+    def spread_y(buffer, number):
+        for layer in range(layers):
+            for comp in range(comps):
+                field = step_y[comp, layer]
+                plus, minus = y_pair(field, turned_edge(edge[number + comp], layer))
+                buffer[comp, layer + 1, TOP:end, :] = field + along_y[comp] * (plus + minus)
+
     def share_end(member):
         slot = members * ens + member
         empty = jnp.zeros((wide, cols), jnp.float32)
@@ -586,9 +587,7 @@
                 field_a[comp, layer] = main
                 all_residual[slot, comp, layer] = residual
                 total = total + own_sum(residual * residual)
-                field = root * residual
-                plus, minus = y_pair(field, turned_edge(edge[EDGE_1 + comp], layer))
-                tq[comp, layer + 1, TOP:end, :] = field + along_y[comp] * (plus + minus)
+                step_y[comp, layer] = root * residual
             return tuple(now), tuple(after), total
 
         nothing = jnp.zeros((8, cols), jnp.float32)
@@ -599,6 +598,7 @@
             _, _, gram_rr = lax.fori_loop(
                 0, layers, residual_layer, ((empty,) * 4, first, nothing), unroll=UNROLL
             )
+            spread_y(tq, EDGE_1)
 
         def image_layer(layer, carry):
             before, now, total_ra, total_aa = carry
@@ -614,9 +614,7 @@
                 all_image[slot, comp, layer] = image
                 total_ra = total_ra + own_sum(residual * image)
                 total_aa = total_aa + own_sum(image * image)
-                field = root * image
-                plus, minus = y_pair(field, turned_edge(edge[EDGE_2 + comp], layer))
-                tp[comp, layer + 1, TOP:end, :] = field + along_y[comp] * (plus + minus)
+                step_y[comp, layer] = root * image
             return tuple(now), tuple(after), total_ra, total_aa
 
         first = tuple(x_sum(tq, comp, 1) for comp in range(comps))
@@ -628,6 +626,7 @@
                 ((empty,) * 2, first, nothing, nothing),
                 unroll=UNROLL,
             )
+            spread_y(tp, EDGE_2)
 
         def own_x_sum(comp, layer):
             return tp[comp, layer, OWN : OWN + rows, :] + along_x[comp] * (
@@ -683,8 +682,16 @@
             arrived(1 + member)
         with scope("q0_start"):
             strip_start(member)
+            if member == 0:
+                arrived(1 + members)
             share_start(member)
         if member == 0:
+            with scope("p5_greeted2"):
+                greeted_round(2)
+            greet_round(4)
+            pl.semaphore_signal(
+                hand_sem.at[len(hands)], inc=1, device_id=partner, device_id_type=MESH
+            )
             arrived(1)
             forces()
         with scope("q1_end"):
@@ -868,7 +875,7 @@
             vmem((planes, 1, cols), f32),
             dma((members + 2,)),
             dma((1,)),
-            dma((1 + members,)),
+            dma((2 + members,)),
             pltpu.SemaphoreType.REGULAR((6,)),
             dma((1,)),
             dma((1,)),

time: 63.6 us -> 63.5 us (level)
  no operation moved by 1% of the time
where the time goes in v6:
time: 63.5 us; the launch traced here: 63.4 us
  Pallas kernels  62.7 us (99%)
  local copies, waits for them, and re-layouts  0.67 us (1%)
    pallas_call x1, Pallas kernels, body(): pl.pallas_call(functools.partial(kernel, sizes), out_shape=jax.ShapeDtype...  62.7 us

profile of v6, /device:TPU:80, one launch (start us, length us, event | category | flops | bytes accessed | tf_op | source)
XLA Modules:
  0.0 63.4 jit_solution(16863687683954401149)
XLA Ops:
  0.0 62.7 %shard_map.55 = f32[2,10,16,128]{3,2,1,0:T(8,128)S(1)} custom-call(f32[2,2,10,16,128]{4,3,2,1,0:T(8,128)} %u_hbm.1, s32[2]{0:T(128)} %picks_hbm.1, f32[16,16,128]{2,1,0:T(8,128)} %table_hbm.1, s32[16,128]{1,0:T(8,128)} %bed_hbm.1, s32[16,128]{1,0:T(8,128)} %mask_hbm.1), custom_call_target="tpu_custom_call" | custom-call | tf_op jit(solution)/shard_map/pallas_call | solution.py:842
  62.7 0.7 %copy.7 = f32[2,10,16,128]{3,2,1,0:T(8,128)} copy(f32[2,10,16,128]{3,2,1,0:T(8,128)S(1)} %shard_map.55) | data formatting | bytes 327680

commit v7 on v6

--- a/solution.py
+++ b/solution.py
@@ -742,7 +742,6 @@
         message,
     )
 
-    share_member(members - 1)
     for comp in range(comps):
         for layer in range(layers):
             total = None
@@ -750,7 +749,6 @@
                 start = mw[0, OWN : OWN + rows, :] * uw[member, comp, layer + 1, OWN : OWN + rows, :]
                 total = start if total is None else total + start
             all_start[ens, comp, layer] = total
-    to_partner(all_start.at[ens])
     everything = {
         name: sum(counts[name] for counts in rows_of) for name in ("x", "y", "both")
     }
@@ -772,6 +770,8 @@
         jnp.sum(ring_y[...], axis=0),
         sign=1,
     )
+    share_member(members - 1)
+    to_partner(all_start.at[ens])
     copies_y.wait_send()
     block = all_residual.at[:, :, :, pl.ds(0, (2 * members + 1) * rows // (2 * members)), :]
     fields = pltpu.make_async_remote_copy(

time: 63.5 us -> 63.5 us (level)
  no operation moved by 1% of the time
where the time goes in v7:
time: 63.5 us; the launch traced here: 63.4 us
  Pallas kernels  62.7 us (99%)
  local copies, waits for them, and re-layouts  0.67 us (1%)
    pallas_call x1, Pallas kernels, body(): pl.pallas_call(functools.partial(kernel, sizes), out_shape=jax.ShapeDtype...  62.7 us

profile of v7, /device:TPU:80, one launch (start us, length us, event | category | flops | bytes accessed | tf_op | source)
XLA Modules:
  0.0 63.4 jit_solution(8471800026425205783)
XLA Ops:
  0.0 62.7 %shard_map.55 = f32[2,10,16,128]{3,2,1,0:T(8,128)S(1)} custom-call(f32[2,2,10,16,128]{4,3,2,1,0:T(8,128)} %u_hbm.1, s32[2]{0:T(128)} %picks_hbm.1, f32[16,16,128]{2,1,0:T(8,128)} %table_hbm.1, s32[16,128]{1,0:T(8,128)} %bed_hbm.1, s32[16,128]{1,0:T(8,128)} %mask_hbm.1), custom_call_target="tpu_custom_call" | custom-call | tf_op jit(solution)/shard_map/pallas_call | solution.py:842
  62.7 0.7 %copy.7 = f32[2,10,16,128]{3,2,1,0:T(8,128)} copy(f32[2,10,16,128]{3,2,1,0:T(8,128)S(1)} %shard_map.55) | data formatting | bytes 327680

commit v8 on v6

--- a/solution.py
+++ b/solution.py
@@ -286,6 +286,7 @@
         load_u[0].wait()
     with scope("p1_barrier"):
         pl.semaphore_wait(barrier, len(around) + 1)
+    greet_round(1)
     block = tally.at[pl.ds(0, maps_rows)]
     pltpu.make_async_copy(block, block, local_sem.at[members + 1]).wait()
     load_picks.wait()
@@ -296,7 +297,6 @@
     pack_u(0)
     send_packed(0, 0, 1 + comps, 0, 1)
     send_u(1 + members, 0)
-    greet_round(1)
     mw[1, OWN : OWN + rows, :] = bed_own
     xo[bed_field, OWN : OWN + rows, :] = lane_packed(lambda layer: bed_own)
     for member in range(members):

time: 63.5 us -> 63.5 us (level)
  no operation moved by 1% of the time
where the time goes in v8:
time: 63.5 us; the launch traced here: 63.4 us
  Pallas kernels  62.7 us (99%)
  local copies, waits for them, and re-layouts  0.67 us (1%)
    pallas_call x1, Pallas kernels, body(): pl.pallas_call(functools.partial(kernel, sizes), out_shape=jax.ShapeDtype...  62.7 us

profile of v8, /device:TPU:80, one launch (start us, length us, event | category | flops | bytes accessed | tf_op | source)
XLA Modules:
  0.0 63.4 jit_solution(7983404474335328274)
XLA Ops:
  0.0 62.7 %shard_map.55 = f32[2,10,16,128]{3,2,1,0:T(8,128)S(1)} custom-call(f32[2,2,10,16,128]{4,3,2,1,0:T(8,128)} %u_hbm.1, s32[2]{0:T(128)} %picks_hbm.1, f32[16,16,128]{2,1,0:T(8,128)} %table_hbm.1, s32[16,128]{1,0:T(8,128)} %bed_hbm.1, s32[16,128]{1,0:T(8,128)} %mask_hbm.1), custom_call_target="tpu_custom_call" | custom-call | tf_op jit(solution)/shard_map/pallas_call | solution.py:842
  62.7 0.7 %copy.7 = f32[2,10,16,128]{3,2,1,0:T(8,128)} copy(f32[2,10,16,128]{3,2,1,0:T(8,128)S(1)} %shard_map.55) | data formatting | bytes 327680
